TPU v7x, 16 devices: a whole 2x2x2 slice. The times are simulated.
16 devices in a mesh: vp: 2 (over z), dp: 8 (over y, x, core).
Axes of the slice: x: 2, y: 2, z: 2, core: 2. Of those that a mesh axis runs over, the one named last changes fastest.
Arguments:
- student_x: bfloat16 [1280, 1536], P('dp')
- teacher_x: bfloat16 [256, 1536], P('dp')
- w_in: bfloat16 [1536, 2048], replicated
- b_in: bfloat16 [2048], replicated
- w_mid: bfloat16 [2048, 2048], replicated
- b_mid: bfloat16 [2048], replicated
- w_out: bfloat16 [2048, 384], replicated
- b_out: bfloat16 [384], replicated
- protos: bfloat16 [384, 131072], P(None, 'vp')
- ema_w_in: bfloat16 [1536, 2048], replicated
- ema_b_in: bfloat16 [2048], replicated
- ema_w_mid: bfloat16 [2048, 2048], replicated
- ema_b_mid: bfloat16 [2048], replicated
- ema_w_out: bfloat16 [2048, 384], replicated
- ema_b_out: bfloat16 [384], replicated
- ema_protos: bfloat16 [384, 131072], P(None, 'vp')
Outputs:
- output 1: float32 [], replicated
- output 2: float32 [1536, 2048], replicated
- output 3: float32 [2048], replicated
- output 4: float32 [2048, 2048], replicated
- output 5: float32 [2048], replicated
- output 6: float32 [2048, 384], replicated
- output 7: float32 [384], replicated
- output 8: float32 [384, 131072], P(None, 'vp')
All inputs are finite; a program needn't handle non-finite values.
Results may differ from a plain program's by a relative error of at most 0.00516174.
Values sent between devices are 32-bit elements.
A program may use at most 1 GiB of HBM per device.

v0:
```python
import functools

import jax
import jax.numpy as jnp
from jax import lax
from jax.experimental import pallas as pl
from jax.experimental.pallas import tpu as pltpu
from jax.sharding import PartitionSpec as P

ALL_CROPS = 10
GLOBAL_CROPS = 2
TEMP_STUDENT = 0.1
TEMP_TEACHER = 0.04
LOG2E = 1.4426950408889634
LANES = 128
NB_A = 512
NB_B = 1024
OUT_SLOTS = 3
HB = 256
F32 = jnp.float32
BF16 = jnp.bfloat16
MESH = pl.DeviceIdType.MESH
HBM = pl.BlockSpec(memory_space=pl.ANY)
VMEM = pl.BlockSpec(memory_space=pltpu.VMEM)


def mlp_forward(feats, w_in, b_in, w_mid, b_mid, w_out, b_out):
    pre_one = jnp.dot(feats, w_in, preferred_element_type=F32) + b_in.astype(F32)
    hid_one = jax.nn.gelu(pre_one, approximate=False).astype(BF16)
    pre_two = jnp.dot(hid_one, w_mid, preferred_element_type=F32) + b_mid.astype(F32)
    hid_two = jax.nn.gelu(pre_two, approximate=False).astype(BF16)
    proj = jnp.dot(hid_two, w_out, preferred_element_type=F32) + b_out.astype(F32)
    inv_norm = lax.rsqrt(jnp.sum(proj * proj, axis=-1, keepdims=True))
    return proj * inv_norm


def unit_columns(block):
    block_f = block.astype(F32)
    inv_col = lax.rsqrt(jnp.sum(block_f * block_f, axis=0, keepdims=True))
    return block_f * inv_col, inv_col


def dot(left, right):
    return jnp.dot(left, right, preferred_element_type=F32)


def dot_t(left, right):
    return lax.dot_general(left, right, (((1,), (1,)), ((), ())), preferred_element_type=F32)


def to_column(row):
    return jnp.transpose(jnp.broadcast_to(row, (LANES, row.shape[1])))


def to_row(acc):
    return jnp.sum(jnp.transpose(acc), axis=0, keepdims=True)


def fold_lanes(wide):
    total = wide[:, :LANES]
    for start in range(LANES, wide.shape[1], LANES):
        total = total + wide[:, start:start + LANES]
    return total


def my_place():
    return lax.axis_index('vp'), lax.axis_index('dp')


def gather_kernel(n_dp, block_ref, all_ref, out_sem, in_sem, fwd_out, fwd_in):
    vp, me = my_place()
    n_chip = n_dp // 2
    chip, core = me // 2, me % 2
    partner = chip * 2 + 1 - core
    n_row = block_ref.shape[1]

    def part(slot):
        return all_ref.at[:, pl.ds(pl.multiple_of(slot * n_row, n_row), n_row)]

    barrier = pltpu.get_barrier_semaphore()
    pl.semaphore_signal(barrier, inc=1, device_id=(vp, partner), device_id_type=MESH)
    for k in range(1, n_chip):
        peer = ((chip + k) % n_chip) * 2 + core
        pl.semaphore_signal(barrier, inc=1, device_id=(vp, peer), device_id_type=MESH)
    pl.semaphore_wait(barrier, n_chip)
    sends = []
    for k in range(1, n_chip):
        peer = ((chip + k) % n_chip) * 2 + core
        sends.append(pltpu.make_async_remote_copy(
            src_ref=block_ref, dst_ref=part(me), send_sem=out_sem.at[k], recv_sem=in_sem.at[chip],
            device_id=(vp, peer), device_id_type=MESH))
    own = pltpu.make_async_remote_copy(
        src_ref=block_ref, dst_ref=part(me), send_sem=fwd_out.at[chip], recv_sem=fwd_in.at[chip],
        device_id=(vp, partner), device_id_type=MESH)
    for copy in sends:
        copy.start()
    own.start()
    all_ref[:, pl.ds(pl.multiple_of(me * n_row, n_row), n_row)] = block_ref[...]
    for k in range(1, n_chip):
        src = (chip + n_chip - k) % n_chip
        slot = src * 2 + core
        peer_copy = pltpu.make_async_remote_copy(
            src_ref=block_ref, dst_ref=part(slot), send_sem=out_sem.at[k], recv_sem=in_sem.at[src],
            device_id=(vp, partner), device_id_type=MESH)
        peer_copy.wait_recv()
        forward = pltpu.make_async_remote_copy(
            src_ref=part(slot), dst_ref=part(slot), send_sem=fwd_out.at[src], recv_sem=fwd_in.at[src],
            device_id=(vp, partner), device_id_type=MESH)
        forward.start()
    for copy in sends:
        copy.wait_send()
    for src in range(n_chip):
        slot = src * 2 + core
        other = src * 2 + 1 - core
        pltpu.make_async_remote_copy(
            src_ref=part(slot), dst_ref=part(other), send_sem=fwd_out.at[src], recv_sem=fwd_in.at[src],
            device_id=(vp, partner), device_id_type=MESH).wait()


def gather_dp(block, n_dp, collective_id):
    groups, n_row, width = block.shape
    return pl.pallas_call(
        functools.partial(gather_kernel, n_dp),
        out_shape=jax.ShapeDtypeStruct((groups, n_row * n_dp, width), block.dtype),
        in_specs=[VMEM],
        out_specs=VMEM,
        scratch_shapes=[pltpu.SemaphoreType.DMA((n_dp // 2,))] * 4,
        compiler_params=pltpu.CompilerParams(
            collective_id=collective_id, has_side_effects=True, vmem_limit_bytes=48 << 20),
        name="gather_dp",
    )(block)


def stats_kernel(n_vp, n_dp, zs_ref, zt_ref, v_hbm, vt_hbm, c_ref, rs_ref, r_ref, ge_ref, loss_ref,
                 vbuf, tbuf, in_sem, ubuf, kbuf, acc_s, acc_r, wbuf, snd, rcv, send_sem, recv_sem, c_out, c_in):
    vp, dp = my_place()
    n_dev = n_vp * n_dp
    me = vp * n_dp + dp
    rows, rows_t = zs_ref.shape[0], zt_ref.shape[0]
    n_img = rows // ALL_CROPS
    n_col = kbuf.shape[1]
    n_blk = n_col // NB_A
    base = dp * n_col

    barrier = pltpu.get_barrier_semaphore()
    for k in range(1, n_dev):
        peer = (me + k) % n_dev
        pl.semaphore_signal(barrier, inc=1, device_id=(peer // n_dp, peer % n_dp), device_id_type=MESH)

    def load(j, slot):
        cols = pl.ds(pl.multiple_of(base + j * NB_A, NB_A), NB_A)
        return (pltpu.make_async_copy(v_hbm.at[:, cols], vbuf.at[slot], in_sem.at[0, slot]),
                pltpu.make_async_copy(vt_hbm.at[:, cols], tbuf.at[slot], in_sem.at[1, slot]))

    for copy in load(0, 0):
        copy.start()
    acc_s[...] = jnp.zeros_like(acc_s)
    acc_r[...] = jnp.zeros_like(acc_r)
    ge_ref[...] = jnp.zeros_like(ge_ref)

    @pl.loop(0, n_blk)
    def _(j):
        slot = j % 2

        @pl.when(j + 1 < n_blk)
        def _():
            for copy in load(j + 1, 1 - slot):
                copy.start()

        for copy in load(j, slot):
            copy.wait()
        here = pl.ds(pl.multiple_of(j * NB_A, NB_A), NB_A)
        unit_t = unit_columns(tbuf[slot])[0].astype(BF16)
        kern = jnp.exp2(dot(zt_ref[...], unit_t) * (LOG2E / TEMP_TEACHER))
        kbuf[:, here] = kern
        acc_r[...] += fold_lanes(kern * (1.0 / jnp.sum(kern, axis=0, keepdims=True)))
        unit = unit_columns(vbuf[slot])[0].astype(BF16)
        ubuf[:, here] = unit
        exp_s = jnp.exp2(dot(zs_ref[...], unit) * (LOG2E / TEMP_STUDENT))
        acc_s[...] += fold_lanes(exp_s)
        ge_ref[...] += dot_t(exp_s.astype(BF16), unit)

    pl.semaphore_wait(barrier, n_dev - 1)

    def exchange(step, width):
        def copy(k, dst, peer):
            return pltpu.make_async_remote_copy(
                src_ref=snd.at[step, :, :width], dst_ref=rcv.at[step, dst, :, :width],
                send_sem=send_sem.at[step, k], recv_sem=recv_sem.at[step, dst],
                device_id=(peer // n_dp, peer % n_dp), device_id_type=MESH)
        for k in range(1, n_dev):
            copy(k, me, (me + k) % n_dev).start()
        rcv[step, me, :, :width] = snd[step, :, :width]
        for k in range(1, n_dev):
            src = (me + n_dev - k) % n_dev
            copy(k, src, src).wait()
        total = rcv[step, 0, :, :width]
        for k in range(1, n_dev):
            total = total + rcv[step, k, :, :width]
        return total

    snd[0, :, :rows_t] = to_row(acc_r[...])
    snd[0, :, rows_t:rows_t + rows] = to_row(acc_s[...])
    total = exchange(0, rows_t + rows)
    row_sum = total[:, rows_t:]
    rs_ref[...] = row_sum
    r_row = 1.0 / total[:, :rows_t]

    for step in (1, 2):
        r_col = to_column(r_row)
        acc_r[...] = jnp.zeros_like(acc_r)

        @pl.loop(0, n_col // LANES)
        def _(j):
            here = pl.ds(pl.multiple_of(j * LANES, LANES), LANES)
            kern = kbuf[:, here]
            c_row = 1.0 / jnp.sum(kern * r_col, axis=0, keepdims=True)
            acc_r[...] += kern * c_row
            if step == 2:
                c_ref[dp, :, here] = c_row

        if step == 2:
            for k in range(1, n_dp):
                pltpu.make_async_remote_copy(
                    src_ref=c_ref.at[dp], dst_ref=c_ref.at[dp], send_sem=c_out.at[k], recv_sem=c_in.at[dp],
                    device_id=(vp, (dp + k) % n_dp), device_id_type=MESH).start()
        snd[step, :, :rows_t] = to_row(acc_r[...])
        r_row = 1.0 / exchange(step, rows_t)
    r_ref[...] = r_row

    r_col = to_column(r_row)
    r_wide = jnp.concatenate([r_col] * (NB_A // LANES), axis=1)
    wbuf[...] = jnp.zeros_like(wbuf)

    @pl.loop(0, n_blk)
    def _(j):
        here = pl.ds(pl.multiple_of(j * NB_A, NB_A), NB_A)
        q_mat = kbuf[:, here] * c_ref[dp, :, here] * r_wide
        q_hi = q_mat.astype(BF16)
        q_lo = (q_mat - q_hi.astype(F32)).astype(BF16)
        unit = ubuf[:, here]
        wbuf[...] += dot_t(q_hi, unit) + dot_t(q_lo, unit)

    w_zero = wbuf[:n_img]
    w_one = wbuf[n_img:]
    w_both = w_zero + w_one
    scale = 1.0 / (n_img * GLOBAL_CROPS * (ALL_CROPS - 1))
    log_rs = jnp.log(row_sum)
    inv_rs = to_column(1.0 / row_sum)
    loss = jnp.zeros((1, LANES), F32)
    for v in range(ALL_CROPS):
        block = pl.ds(v * n_img, n_img)
        count = float(GLOBAL_CROPS - (v < GLOBAL_CROPS))
        w_v = (w_one, w_zero)[v] if v < GLOBAL_CROPS else w_both
        inv = inv_rs[v * n_img:(v + 1) * n_img]
        inv = jnp.concatenate([inv] * (ge_ref.shape[1] // LANES), axis=1)
        dots = fold_lanes(jnp.sum(zs_ref[block].astype(F32) * w_v, axis=0, keepdims=True))
        logs = log_rs[:, v * n_img:(v + 1) * n_img]
        loss += (count / n_dev) * logs - (1.0 / TEMP_STUDENT) * dots
        ge_ref[block] = (count * (ge_ref[block] * inv) - w_v) * (scale / TEMP_STUDENT)
    loss_ref[...] = loss * scale

    for k in range(1, n_dp):
        src = (dp + n_dp - k) % n_dp
        pltpu.make_async_remote_copy(
            src_ref=c_ref.at[dp], dst_ref=c_ref.at[src], send_sem=c_out.at[k], recv_sem=c_in.at[src],
            device_id=(vp, src), device_id_type=MESH).wait()


def sinkhorn_stats(z_s, z_t, protos, ema_protos, n_vp, n_dp):
    rows, width = z_s.shape
    rows_t = z_t.shape[0]
    n_col = protos.shape[1] // n_dp
    n_dev = n_vp * n_dp
    flops = 2 * rows * n_col * width * 2
    return pl.pallas_call(
        functools.partial(stats_kernel, n_vp, n_dp),
        out_shape=(jax.ShapeDtypeStruct((n_dp, 1, n_col), F32),
                   jax.ShapeDtypeStruct((1, rows), F32),
                   jax.ShapeDtypeStruct((1, rows_t), F32),
                   jax.ShapeDtypeStruct((rows, width), F32),
                   jax.ShapeDtypeStruct((1, LANES), F32)),
        in_specs=[VMEM, VMEM, HBM, HBM],
        out_specs=(VMEM,) * 5,
        scratch_shapes=[
            pltpu.VMEM((2, width, NB_A), BF16),
            pltpu.VMEM((2, width, NB_A), BF16),
            pltpu.SemaphoreType.DMA((2, 2)),
            pltpu.VMEM((width, n_col), BF16),
            pltpu.VMEM((rows_t, n_col), F32),
            pltpu.VMEM((rows, LANES), F32),
            pltpu.VMEM((rows_t, LANES), F32),
            pltpu.VMEM((rows_t, width), F32),
            pltpu.VMEM((3, 1, rows + rows_t), F32),
            pltpu.VMEM((3, n_dev, 1, rows + rows_t), F32),
            pltpu.SemaphoreType.DMA((3, n_dev)),
            pltpu.SemaphoreType.DMA((3, n_dev)),
            pltpu.SemaphoreType.DMA((n_dp,)),
            pltpu.SemaphoreType.DMA((n_dp,)),
        ],
        compiler_params=pltpu.CompilerParams(
            collective_id=1, has_side_effects=True, vmem_limit_bytes=60 << 20),
        cost_estimate=pl.CostEstimate(flops=flops, bytes_accessed=4 * width * n_col, transcendentals=rows * n_col),
        name="sinkhorn_stats",
    )(z_s, z_t, protos, ema_protos)


def grads_kernel(n_vp, n_dp, zs_ref, zst_ref, zt_ref, rs_ref, r_ref, c_ref, ge_ref, loss_ref, x_ref, v_hbm, vt_hbm,
                 g_hbm, ge_all, loss_all, x_all, vbuf, tbuf, obuf, part_ge, sum_ge, part_loss, in_sem, loc_sem, out_sem,
                 recv_sem, rs_out, rs_in, ag_out, ag_in, ls_out, ls_in, x_out, x_in, xf_out, xf_in, x_own):
    vp, dp = my_place()
    n_dev = n_vp * n_dp
    me = vp * n_dp + dp
    n_chip = n_dp // 2
    chip, core = dp // 2, dp % 2
    partner = chip * 2 + 1 - core
    rows, rows_t = zs_ref.shape[0], zt_ref.shape[0]
    n_img = rows // ALL_CROPS
    n_own = rows // n_dev
    n_loc = x_ref.shape[1]
    half = v_hbm.shape[1] // 2
    n_slice = c_ref.shape[2]
    n_blk = half // NB_B
    base = core * half
    barrier = pltpu.get_barrier_semaphore()
    for k in range(1, n_dev):
        peer = (me + k) % n_dev
        pl.semaphore_signal(barrier, inc=1, device_id=(peer // n_dp, peer % n_dp), device_id_type=MESH)

    def load(j, slot):
        cols = pl.ds(pl.multiple_of(base + j * NB_B, NB_B), NB_B)
        return (pltpu.make_async_copy(v_hbm.at[:, cols], vbuf.at[slot], in_sem.at[0, slot]),
                pltpu.make_async_copy(vt_hbm.at[:, cols], tbuf.at[slot], in_sem.at[1, slot]))

    def local_store(j):
        slot = j % OUT_SLOTS
        cols = pl.ds(pl.multiple_of(base + j * NB_B, NB_B), NB_B)
        return pltpu.make_async_copy(obuf.at[slot], g_hbm.at[:, cols], loc_sem.at[slot])

    def remote_store(j):
        slot = j % OUT_SLOTS
        cols = pl.ds(pl.multiple_of(base + j * NB_B, NB_B), NB_B)
        return pltpu.make_async_remote_copy(
            src_ref=obuf.at[slot], dst_ref=g_hbm.at[:, cols], send_sem=out_sem.at[slot],
            recv_sem=recv_sem.at[j], device_id=(vp, partner), device_id_type=MESH)

    def peer_of(k):
        peer = (me + k) % n_dev
        return peer, (peer // n_dp, peer % n_dp)

    def scatter(k, peer, dst, device):
        return pltpu.make_async_remote_copy(
            src_ref=ge_ref.at[pl.ds(pl.multiple_of(peer * n_own, n_own), n_own)], dst_ref=part_ge.at[dst],
            send_sem=rs_out.at[k], recv_sem=rs_in.at[dst], device_id=device, device_id_type=MESH)

    def spread(k, owner, device):
        return pltpu.make_async_remote_copy(
            src_ref=sum_ge, dst_ref=ge_all.at[pl.ds(pl.multiple_of(owner * n_own, n_own), n_own)],
            send_sem=ag_out.at[k], recv_sem=ag_in.at[owner], device_id=device, device_id_type=MESH)

    def loss_send(k, dst, device):
        return pltpu.make_async_remote_copy(
            src_ref=loss_ref, dst_ref=part_loss.at[dst], send_sem=ls_out.at[k], recv_sem=ls_in.at[dst],
            device_id=device, device_id_type=MESH)

    def x_part(slot):
        return x_all.at[:, pl.ds(pl.multiple_of(slot * n_loc, n_loc), n_loc)]

    def x_send(k, src_chip, slot, device):
        return pltpu.make_async_remote_copy(
            src_ref=x_ref, dst_ref=x_part(slot), send_sem=x_out.at[k], recv_sem=x_in.at[src_chip],
            device_id=device, device_id_type=MESH)

    def x_forward(src_chip, slot):
        return pltpu.make_async_remote_copy(
            src_ref=x_part(slot), dst_ref=x_part(slot), send_sem=xf_out.at[src_chip], recv_sem=xf_in.at[src_chip],
            device_id=(vp, partner), device_id_type=MESH)

    for copy in load(0, 0):
        copy.start()
    x_local = pltpu.make_async_copy(x_ref, x_part(dp), x_own.at[0])
    x_local.start()
    scale = 1.0 / (n_img * GLOBAL_CROPS * (ALL_CROPS - 1)) / TEMP_STUDENT
    lanes = lax.broadcasted_iota(jnp.int32, (1, rows), 1)
    weight = jnp.where(lanes < GLOBAL_CROPS * n_img, scale, GLOBAL_CROPS * scale)
    bias = to_column(jnp.log(weight / rs_ref[...]) * LOG2E)
    bias = jnp.concatenate([bias] * (NB_B // LANES), axis=1)
    r_col = to_column(r_ref[...] * scale)
    r_wide = jnp.concatenate([r_col] * (NB_B // LANES), axis=1)
    pl.semaphore_wait(barrier, n_dev - 1)
    for k in range(1, n_dev):
        peer, device = peer_of(k)
        loss_send(k, me, device).start()
        scatter(k, peer, me, device).start()
    for k in range(1, n_chip):
        x_send(k, chip, dp, (vp, ((chip + k) % n_chip) * 2 + core)).start()
    part_ge[me] = ge_ref[pl.ds(pl.multiple_of(me * n_own, n_own), n_own)]
    part_loss[me] = loss_ref[...]

    @pl.loop(0, n_blk)
    def _(j):
        slot = j % 2

        @pl.when(j + 1 < n_blk)
        def _():
            for copy in load(j + 1, 1 - slot):
                copy.start()

        @pl.when(j >= 1)
        def _():
            local_store(j - 1).start()
            remote_store(j - 1).start()

        @pl.when(j >= OUT_SLOTS)
        def _():
            local_store(j - OUT_SLOTS).wait()
            remote_store(j - OUT_SLOTS).wait_send()

        @pl.when(j == n_blk // 2)
        def _():
            for k in range(1, n_dev):
                src = (me + n_dev - k) % n_dev
                scatter(k, src, src, (vp, partner)).wait()
                loss_send(k, src, (vp, partner)).wait()
            total = part_ge[0]
            loss = part_loss[0]
            for k in range(1, n_dev):
                total = total + part_ge[k]
                loss = loss + part_loss[k]
            loss_all[...] = loss
            sum_ge[...] = total
            ge_all[pl.ds(pl.multiple_of(me * n_own, n_own), n_own)] = total

        @pl.when(j == n_blk // 2 + 1)
        def _():
            for k in range(1, n_dev):
                spread(k, me, peer_of(k)[1]).start()

        @pl.when(j == n_blk - 4)
        def _():
            x_local.wait()
            x_forward(chip, dp).start()
            for k in range(1, n_chip):
                src = (chip + n_chip - k) % n_chip
                x_send(k, src, src * 2 + core, (vp, partner)).wait()
                x_forward(src, src * 2 + core).start()

        for copy in load(j, slot):
            copy.wait()
        unit_t = unit_columns(tbuf[slot])[0].astype(BF16)
        col = base + j * NB_B
        c_row = c_ref[col // n_slice, :, pl.ds(pl.multiple_of(col % n_slice, NB_B), NB_B)]
        q_mat = jnp.exp2(dot(zt_ref[...], unit_t) * (LOG2E / TEMP_TEACHER)) * c_row * r_wide
        q_zero, q_one = q_mat[:n_img], q_mat[n_img:]
        q_both = q_zero + q_one
        unit, inv_col = unit_columns(vbuf[slot])
        logits = dot(zs_ref[...], unit.astype(BF16))
        soft = jnp.exp2(logits * (LOG2E / TEMP_STUDENT) + bias)
        target = jnp.concatenate([q_one, q_zero] + [q_both] * (ALL_CROPS - GLOBAL_CROPS), axis=0)
        g_unit = dot(zst_ref[...], (soft - target).astype(BF16))
        obuf[j % OUT_SLOTS] = (g_unit - unit * jnp.sum(unit * g_unit, axis=0, keepdims=True)) * inv_col

    local_store(n_blk - 1).start()
    remote_store(n_blk - 1).start()
    for j in range(n_blk - OUT_SLOTS, n_blk):
        local_store(j).wait()
        remote_store(j).wait_send()
    for k in range(1, n_dev):
        src = (me + n_dev - k) % n_dev
        spread(k, src, (vp, partner)).wait()
    for src in range(n_chip):
        pltpu.make_async_remote_copy(
            src_ref=x_part(src * 2 + core), dst_ref=x_part(src * 2 + 1 - core), send_sem=xf_out.at[src],
            recv_sem=xf_in.at[src], device_id=(vp, partner), device_id_type=MESH).wait()

    @pl.loop(0, n_blk)
    def _(j):
        remote_store(j).wait_recv()


def proto_grads(z_s, z_t, row_sum, r_row, c_all, g_emb, loss, x_loc, protos, ema_protos, n_vp, n_dp):
    rows, width = z_s.shape
    n_col = protos.shape[1]
    n_blk = n_col // 2 // NB_B
    n_dev = n_vp * n_dp
    dma = pltpu.SemaphoreType.DMA
    return pl.pallas_call(
        functools.partial(grads_kernel, n_vp, n_dp),
        out_shape=(jax.ShapeDtypeStruct((width, n_col), F32),
                   jax.ShapeDtypeStruct((rows, width), F32),
                   jax.ShapeDtypeStruct((1, LANES), F32),
                   jax.ShapeDtypeStruct((x_loc.shape[0], x_loc.shape[1] * n_dp, x_loc.shape[2]), F32)),
        in_specs=[VMEM] * 9 + [HBM] * 2,
        out_specs=(HBM, VMEM, VMEM, HBM),
        scratch_shapes=[
            pltpu.VMEM((2, width, NB_B), BF16),
            pltpu.VMEM((2, width, NB_B), BF16),
            pltpu.VMEM((OUT_SLOTS, width, NB_B), F32),
            pltpu.VMEM((n_dev, rows // n_dev, width), F32),
            pltpu.VMEM((rows // n_dev, width), F32),
            pltpu.VMEM((n_dev, 1, LANES), F32),
            dma((2, 2)),
            dma((OUT_SLOTS,)),
            dma((OUT_SLOTS,)),
            dma((n_blk,)),
        ] + [dma((n_dev,))] * 6 + [dma((n_dp // 2,))] * 4 + [dma((1,))],
        compiler_params=pltpu.CompilerParams(
            collective_id=2, has_side_effects=True, vmem_limit_bytes=60 << 20),
        cost_estimate=pl.CostEstimate(
            flops=2 * rows * n_col * width, bytes_accessed=4 * width * n_col, transcendentals=rows * n_col // 2),
        name="proto_grads",
    )(z_s, z_s.T, z_t, row_sum, r_row, c_all, g_emb, loss, x_loc, protos, ema_protos)


def head_kernel(x_hbm, wi_hbm, wm_hbm, wo_hbm, bi_ref, bm_ref, bo_ref, ge_ref,
                h1_hbm, h2_hbm, g2_hbm, g1_hbm, gp_ref, bias_ref,
                x_buf, wi, wm, wo, hid_one, hid_two, slope_one, slope_two, stage, grad_two, gp_stage, snd, rcv,
                ld_sem, loc_sem, out_sem, in_sem, gp_sem, bs_sem):
    vp, dp = my_place()
    chip, core = dp // 2, dp % 2
    partner = chip * 2 + 1 - core
    half, n_hid = hid_one.shape
    n_out = wo.shape[1]
    n_blk = n_hid // HB
    mine = pl.ds(pl.multiple_of(core * half, half), half)
    device = (vp, partner)
    barrier = pltpu.get_barrier_semaphore()
    pl.semaphore_signal(barrier, inc=1, device_id=device, device_id_type=MESH)
    loads = [pltpu.make_async_copy(x_hbm.at[mine], x_buf, ld_sem.at[0]),
             pltpu.make_async_copy(wi_hbm, wi, ld_sem.at[1]),
             pltpu.make_async_copy(wm_hbm, wm, ld_sem.at[2]),
             pltpu.make_async_copy(wo_hbm, wo, ld_sem.at[3])]
    for copy in loads:
        copy.start()
    pl.semaphore_wait(barrier, 1)

    def block(j):
        return pl.ds(pl.multiple_of(j * HB, HB), HB)

    def keep(array, dst, j):
        return pltpu.make_async_copy(
            stage.at[array % 2, :, block(j)], dst.at[mine, block(j)], loc_sem.at[array, j])

    def send(array, dst, j):
        return pltpu.make_async_remote_copy(
            src_ref=stage.at[array % 2, :, block(j)], dst_ref=dst.at[mine, block(j)], send_sem=out_sem.at[array, j],
            recv_sem=in_sem.at[array, j], device_id=device, device_id_type=MESH)

    def flush(array, dst, j):
        keep(array, dst, j).start()
        send(array, dst, j).start()

    def drain(array, dst):
        @pl.loop(0, n_blk)
        def _(j):
            keep(array, dst, j).wait()
            send(array, dst, j).wait_send()

    def layer(array, feats, weight, b_ref, hid, slope, dst):
        @pl.loop(0, n_blk)
        def _(j):
            @pl.when(j >= 1)
            def _():
                flush(array, dst, j - 1)

            pre = dot(feats, weight[:, block(j)]) + b_ref[:, block(j)].astype(F32)
            cdf = 0.5 * (1.0 + lax.erf(pre * 0.7071067811865476))
            low = (pre * cdf).astype(BF16)
            hid[:, block(j)] = low
            stage[array % 2, :, block(j)] = low.astype(F32)
            slope[:, block(j)] = cdf + pre * jnp.exp(-0.5 * pre * pre) * 0.3989422804014327
        flush(array, dst, n_blk - 1)

    loads[0].wait()
    loads[1].wait()
    layer(0, x_buf[...].astype(BF16), wi, bi_ref, hid_one, slope_one, h1_hbm)
    loads[2].wait()
    layer(1, hid_one[...], wm, bm_ref, hid_two, slope_two, h2_hbm)
    loads[3].wait()
    proj = dot(hid_two[...], wo[...]) + bo_ref[...].astype(F32)
    inv_norm = lax.rsqrt(jnp.sum(proj * proj, axis=-1, keepdims=True))
    unit = proj * inv_norm
    g_emb = ge_ref[mine]
    g_proj = (g_emb - unit * jnp.sum(unit * g_emb, axis=-1, keepdims=True)) * inv_norm
    gp_low = g_proj.astype(BF16)
    gp_stage[...] = gp_low.astype(F32)
    gp_ref[mine] = gp_low.astype(F32)
    snd[:, 2 * n_hid:] = jnp.sum(g_proj, axis=0, keepdims=True)
    drain(0, h1_hbm)

    @pl.loop(0, n_blk)
    def _(j):
        @pl.when(j >= 1)
        def _():
            flush(2, g2_hbm, j - 1)

        g_hid = dot_t(gp_low, wo[block(j), :])
        g_pre = g_hid.astype(BF16).astype(F32) * slope_two[:, block(j)]
        snd[:, block(j)] = jnp.sum(g_pre, axis=0, keepdims=True)
        low = g_pre.astype(BF16)
        grad_two[:, block(j)] = low
        stage[0, :, block(j)] = low.astype(F32)
    flush(2, g2_hbm, n_blk - 1)
    gp_send = pltpu.make_async_remote_copy(
        src_ref=gp_stage, dst_ref=gp_ref.at[mine], send_sem=gp_sem.at[0], recv_sem=gp_sem.at[1],
        device_id=device, device_id_type=MESH)
    gp_send.start()
    drain(1, h2_hbm)

    @pl.loop(0, n_blk)
    def _(j):
        @pl.when(j >= 1)
        def _():
            flush(3, g1_hbm, j - 1)

        g_hid = dot_t(grad_two[...], wm[block(j), :])
        g_pre = g_hid.astype(BF16).astype(F32) * slope_one[:, block(j)]
        snd[:, pl.ds(pl.multiple_of(n_hid + j * HB, HB), HB)] = jnp.sum(g_pre, axis=0, keepdims=True)
        stage[1, :, block(j)] = g_pre.astype(BF16).astype(F32)
    flush(3, g1_hbm, n_blk - 1)
    bias_send = pltpu.make_async_remote_copy(
        src_ref=snd, dst_ref=rcv, send_sem=bs_sem.at[0], recv_sem=bs_sem.at[1],
        device_id=device, device_id_type=MESH)
    bias_send.start()
    drain(2, g2_hbm)
    drain(3, g1_hbm)
    gp_send.wait()
    bias_send.wait()
    bias_ref[...] = snd[...] + rcv[...]
    for array, dst in enumerate((h1_hbm, h2_hbm, g2_hbm, g1_hbm)):
        @pl.loop(0, n_blk)
        def _(j):
            send(array, dst, j).wait_recv()


def head_pass(x_all, w_in, b_in, w_mid, b_mid, w_out, b_out, g_emb):
    rows, feat = x_all.shape
    n_hid, n_out = w_out.shape
    half = rows // 2
    n_blk = n_hid // HB
    n_bias = 2 * n_hid + n_out
    dma = pltpu.SemaphoreType.DMA
    wide = jax.ShapeDtypeStruct((rows, n_hid), F32)
    return pl.pallas_call(
        head_kernel,
        out_shape=(wide, wide, wide, wide, jax.ShapeDtypeStruct((rows, n_out), F32),
                   jax.ShapeDtypeStruct((1, n_bias), F32)),
        in_specs=[HBM] * 4 + [VMEM] * 4,
        out_specs=(HBM,) * 4 + (VMEM,) * 2,
        scratch_shapes=[
            pltpu.VMEM((half, feat), F32),
            pltpu.VMEM((feat, n_hid), BF16),
            pltpu.VMEM((n_hid, n_hid), BF16),
            pltpu.VMEM((n_hid, n_out), BF16),
            pltpu.VMEM((half, n_hid), BF16),
            pltpu.VMEM((half, n_hid), BF16),
            pltpu.VMEM((half, n_hid), F32),
            pltpu.VMEM((half, n_hid), F32),
            pltpu.VMEM((2, half, n_hid), F32),
            pltpu.VMEM((half, n_hid), BF16),
            pltpu.VMEM((half, n_out), F32),
            pltpu.VMEM((1, n_bias), F32),
            pltpu.VMEM((1, n_bias), F32),
            dma((4,)), dma((4, n_blk)), dma((4, n_blk)), dma((4, n_blk)), dma((2,)), dma((2,)),
        ],
        compiler_params=pltpu.CompilerParams(
            collective_id=3, has_side_effects=True, vmem_limit_bytes=63 << 20),
        cost_estimate=pl.CostEstimate(
            flops=2 * rows * (feat + 2 * n_hid) * n_hid, bytes_accessed=16 * rows * n_hid, transcendentals=2 * rows * n_hid),
        name="head_pass",
    )(x_all, w_in, w_mid, w_out, b_in.reshape(1, -1), b_mid.reshape(1, -1), b_out.reshape(1, -1), g_emb)


def wgrad_kernel(first, n_step, base, *refs):
    if first:
        a_ref, b_ref, src, out_ref, dst, low, cbuf, rd_sem, wr_sem = refs
    else:
        a_ref, b_ref, src, _, out_ref, dst, low, cbuf, rd_sem, wr_sem = refs
    i = pl.program_id(0)
    chunk = cbuf.shape[2]

    def cols(step):
        return pl.ds(pl.multiple_of(base + step * chunk, chunk), chunk)

    def read(step):
        return pltpu.make_async_copy(src.at[:, cols(step)], cbuf.at[step % 3], rd_sem.at[step % 3])

    def write(step):
        return pltpu.make_async_copy(cbuf.at[step % 3], dst.at[:, cols(step)], wr_sem.at[step % 3])

    @pl.when(i == 0)
    def _():
        read(0).start()
        low[...] = b_ref[...].astype(BF16)

    @pl.when(i >= 2)
    def _():
        write(i - 2).wait()

    @pl.when(i + 1 < n_step)
    def _():
        read(i + 1).start()

    read(i).wait()
    write(i).start()
    out_ref[...] = lax.dot_general(
        a_ref[...].astype(BF16), low[...], (((0,), (0,)), ((), ())), preferred_element_type=F32)

    @pl.when(i == n_step - 1)
    def _():
        write(i - 1).wait()
        write(i).wait()


def wgrad(left, right, src, dst, start, width, block=256):
    rows, n_left = left.shape
    n_right = right.shape[1]
    n_step = n_left // block
    first = dst is None
    chunk = width // n_step
    args = (left, right, src) + (() if first else (dst,))
    return pl.pallas_call(
        functools.partial(wgrad_kernel, first, n_step, start),
        grid=(n_step,),
        out_shape=(jax.ShapeDtypeStruct((n_left, n_right), F32), jax.ShapeDtypeStruct(src.shape, F32)),
        in_specs=[pl.BlockSpec((rows, block), lambda i: (0, i)),
                  pl.BlockSpec((rows, n_right), lambda i: (0, 0), pipeline_mode=pl.Buffered(1)),
                  HBM] + ([] if first else [HBM]),
        out_specs=(pl.BlockSpec((block, n_right), lambda i: (i, 0)), HBM),
        scratch_shapes=[pltpu.VMEM((rows, n_right), BF16),
                        pltpu.VMEM((3, src.shape[0], chunk), F32),
                        pltpu.SemaphoreType.DMA((3,)), pltpu.SemaphoreType.DMA((3,))],
        input_output_aliases={} if first else {3: 1},
        compiler_params=pltpu.CompilerParams(
            dimension_semantics=("arbitrary",), vmem_limit_bytes=60 << 20),
        cost_estimate=pl.CostEstimate(
            flops=2 * rows * n_left * n_right, bytes_accessed=8 * src.shape[0] * width, transcendentals=0),
        name="wgrad",
    )(*args)


def solution(mesh):
    n_vp = mesh.shape['vp']
    n_dp = mesh.shape['dp']

    def local_step(student_x, teacher_x, w_in, b_in, w_mid, b_mid, w_out, b_out, protos,
                   ema_w_in, ema_b_in, ema_w_mid, ema_b_mid, ema_w_out, ema_b_out, ema_protos):
        rows, feat = student_x.shape
        n_img = rows // ALL_CROPS
        width = protos.shape[0]
        x_loc = student_x.reshape(n_img, ALL_CROPS, feat).transpose(1, 0, 2)
        t_loc = teacher_x.reshape(n_img, GLOBAL_CROPS, feat).transpose(1, 0, 2).reshape(-1, feat)
        t_emb = mlp_forward(t_loc, ema_w_in, ema_b_in, ema_w_mid, ema_b_mid, ema_w_out, ema_b_out)
        s_emb = mlp_forward(x_loc.reshape(rows, feat), w_in, b_in, w_mid, b_mid, w_out, b_out)
        z_loc = jnp.concatenate([s_emb, t_emb], axis=0).reshape(ALL_CROPS + GLOBAL_CROPS, n_img, width)
        z_all = gather_dp(z_loc, n_dp, 0).reshape(-1, width).astype(BF16)
        z_s, z_t = z_all[:rows * n_dp], z_all[rows * n_dp:]
        c_all, row_sum, r_row, g_emb, loss = sinkhorn_stats(z_s, z_t, protos, ema_protos, n_vp, n_dp)
        g_temp, g_emb, loss, x_all = proto_grads(
            z_s, z_t, row_sum, r_row, c_all, g_emb, loss, x_loc.astype(F32), protos, ema_protos, n_vp, n_dp)
        x_all = x_all.reshape(rows * n_dp, feat)
        hid_one, hid_two, g_two, g_one, g_proj, biases = head_pass(
            x_all, w_in, b_in, w_mid, b_mid, w_out, b_out, g_emb)
        n_hid = w_mid.shape[0]
        part = protos.shape[1] // 8
        g_w_mid, g_protos = wgrad(hid_one, g_two, g_temp, None, 0, 4 * part)
        g_w_in, g_protos = wgrad(x_all, g_one, g_temp, g_protos, 4 * part, 3 * part)
        g_w_out, g_protos = wgrad(hid_two, g_proj, g_temp, g_protos, 7 * part, part)
        biases = biases.reshape(-1)
        g_b_mid, g_b_in, g_b_out = biases[:n_hid], biases[n_hid:2 * n_hid], biases[2 * n_hid:]
        return (jnp.sum(loss), g_w_in, g_b_in, g_w_mid, g_b_mid, g_w_out, g_b_out, g_protos)

    by_rows = P('dp', None)
    by_cols = P(None, 'vp')
    replicated = P()
    head_specs = (replicated,) * 6
    in_specs = (by_rows, by_rows) + head_specs + (by_cols,) + head_specs + (by_cols,)
    out_specs = (replicated,) * 7 + (by_cols,)
    return jax.shard_map(local_step, mesh=mesh, in_specs=in_specs, out_specs=out_specs, check_vma=False)
```

profile of v0, /device:TPU:0, one launch (start us, length us, event | category | flops | bytes accessed | tf_op | source)
XLA Modules:
  0.0 388.4 jit_solution(10322767374511469405)
XLA Ops:
  0.6 0.7 convert_element_type.46
  1.3 0.9 reshape.67
  2.3 0.7 convert_element_type.42
  3.0 0.0 copy-start.6
  3.0 0.0 copy-start.8
  3.0 4.6 %fusion.56 = bf16[32,2048]{1,0:T(8,128)(2,1)S(1)} fusion(bf16[32,1536]{1,0:T(8,128)(2,1)S(1)} %bitcast.34, bf16[1536,2048]{1,0:T(8,128)(2,1)} %param.25, f32[2048]{0:T(1024)S(1)} %convert_element_type.42), kind=kOutput, calls=%fused_computation.81 | convolution fusion | flops 205651968 | bytes 6529024 | tf_op jit(solution)/shard_map/dot_general | solution.py:28
  7.6 0.0 copy-done.6
  7.6 0.0 copy-done.8
  7.6 0.0 copy-start.7
  7.7 0.0 copy-start.2
  7.7 5.6 %multiply_reduce_fusion.1 = (f32[32]{0:T(128)S(1)}, f32[32,384]{1,0:T(8,128)S(1)}) fusion(f32[384]{0:T(512)S(1)} %convert_element_type.46, bf16[2048,384]{1,0:T(8,128)(2,1)S(1)} %copy-done.8, bf16[32,2048]{1,0:T(8,128)(2,1)S(1)} %fusion.56, bf16[2048,2048]{1,0:T(8,128)(2,1)} %param.27, f32[2048]{0:T(1024)S(1)} %convert_element_type.44), kind=kOutput, calls=%fused_computation.148 | convolution fusion | flops 323129312 | bytes 10151552 | tf_op jit(solution)/shard_map/dot_general | solution.py:32
  13.3 0.1 broadcast_multiply_fusion.1
  13.4 0.0 copy-done.7
  13.4 0.0 copy-done.2
  13.4 0.2 reshape.65
  13.6 0.0 copy-start.5
  13.6 0.0 copy-start.4
  13.6 1.2 bitcast_convert_fusion
  14.8 0.0 copy-done.5
  14.8 0.0 copy-done.4
  14.8 0.0 copy-start.1
  14.9 13.6 %fusion.5 = bf16[160,2048]{1,0:T(8,128)(2,1)S(1)} fusion(bf16[2048,2048]{1,0:T(8,128)(2,1)} %wm_hbm.1, bf16[160,1536]{1,0:T(8,128)(2,1)S(1)} %bitcast.32, bf16[1536,2048]{1,0:T(8,128)(2,1)} %wi_hbm.1, f32[2048]{0:T(1024)S(1)} %convert_element_type.39, f32[2048]{0:T(1024)S(1)} %convert_element_type.37), kind=kOutput, calls=%fused_computation.11 | convolution fusion | flops 2392064000 | bytes 15843328 | tf_op jit(solution)/shard_map/dot_general | solution.py:30
  28.4 0.0 copy-done.1
  28.4 0.8 multiply_reduce_fusion
  29.3 0.1 broadcast_multiply_fusion
  29.4 19.4 %gather_dp.1 = f32[12,128,384]{2,1,0:T(8,128)S(1)} custom-call(f32[12,16,384]{2,1,0:T(8,128)S(1)} %bitcast.23), custom_call_target="tpu_custom_call" | custom-call | tf_op jit(solution)/shard_map/gather_dp/pallas_call | solution.py:122
  48.8 0.2 convert_element_type.47
  49.0 0.1 slice.40
  49.1 0.0 copy-start
  49.1 1.3 copy.33
  50.4 0.7 slice.41
  51.1 0.0 copy-done
  51.1 65.7 %sinkhorn_stats.1 = (f32[8,1,8192]{2,1,0:T(1,128)}, f32[1,1280]{1,0:T(1,128)}, f32[1,256]{1,0:T(1,128)}, f32[1280,384]{1,0:T(8,128)}, f32[1,128]{1,0:T(1,128)}) custom-call(bf16[1280,384]{1,0:T(8,128)(2,1)} %bitcast.25, bf16[256,384]{1,0:T(8,128)(2,1)} %bitcast.30, bf16[384,65536]{1,0:T(8,128)(2,1)} %v_hbm.3, bf16[384,65536]{1,0:T(8,128)(2,1)} %vt_hbm.3), custom_call_target="tpu_custom_call" | custom-call | flops 16106127360 | bytes 12582912 | tf_op jit(solution)/shard_map/sinkhorn_stats/pallas_call | solution.py:276
  116.9 124.3 %proto_grads.1 = (f32[384,65536]{1,0:T(8,128)}, f32[1280,384]{1,0:T(8,128)}, f32[1,128]{1,0:T(1,128)}, f32[10,128,1536]{2,1,0:T(8,128)}) custom-call(bf16[1280,384]{1,0:T(8,128)(2,1)} %bitcast.26, bf16[384,1280]{1,0:T(8,128)(2,1)} %bitcast.29, bf16[256,384]{1,0:T(8,128)(2,1)} %bitcast.31, f32[1,1280]{1,0:T(1,128)} %get-tuple-element.29.rs_ref, ...), custom_call_target="tpu_custom_call" | custom-call | flops 64424509440 | bytes 100663296 | tf_op jit(solution)/shard_map/proto_grads/pallas_call | solution.py:487
  241.2 1.3 reduce_sum.29
  242.5 0.6 reshape.71.bi_ref
  243.1 0.6 reshape.72.bm_ref
  243.7 0.6 reshape.73.bo_ref
  244.3 43.7 %head_pass.1 = (f32[1280,2048]{1,0:T(8,128)}, f32[1280,2048]{1,0:T(8,128)}, f32[1280,2048]{1,0:T(8,128)}, f32[1280,2048]{1,0:T(8,128)}, f32[1280,384]{1,0:T(8,128)}, /*index=5*/f32[1,4480]{1,0:T(1,128)}) custom-call(f32[1280,1536]{1,0:T(8,128)} %bitcast.27, bf16[1536,2048]{1,0:T(8,128)(2,1)} %wi_hbm.1, bf16[2048,2048]{1,0:T(8,128)(2,1)} %wm_hbm.1, ...), custom_call_target="tpu_custom_call" | custom-call | flops 29527900160 | bytes 41943040 | tf_op jit(solution)/shard_map/head_pass/pallas_call | solution.py:644
  288.0 46.6 %wgrad.3 = (f32[2048,2048]{1,0:T(8,128)}, f32[384,65536]{1,0:T(8,128)}) custom-call(f32[1280,2048]{1,0:T(8,128)} %get-tuple-element.39.refs_0_, f32[1280,2048]{1,0:T(8,128)} %get-tuple-element.40.refs_1_, f32[384,65536]{1,0:T(8,128)} %get-tuple-element.38.refs_2_), custom_call_target="tpu_custom_call" | custom-call | flops 10737418240 | bytes 100663296 | tf_op jit(solution)/shard_map/wgrad/pallas_call | solution.py:722
  334.6 0.0 copy-start.3
  334.6 36.2 %wgrad.4 = (f32[1536,2048]{1,0:T(8,128)}, f32[384,65536]{1,0:T(8,128)}) custom-call(f32[1280,1536]{1,0:T(8,128)} %bitcast.28, f32[1280,2048]{1,0:T(8,128)} %get-tuple-element.37.refs_1_, f32[384,65536]{1,0:T(8,128)} %get-tuple-element.38.refs_2_, f32[384,65536]{1,0:T(8,128)} %get-tuple-element.41.refs_3_), custom_call_target="tpu_custom_call", output_to_operand_aliasing={{1}: (3, {})} | custom-call | flops 8053063680 | bytes 75497472 | tf_op jit(solution)/shard_map/wgrad/pallas_call | solution.py:722
  370.8 0.0 copy-done.3
  370.8 0.6 fusion.165
  371.4 16.3 %wgrad.5 = (f32[2048,384]{1,0:T(8,128)}, f32[384,65536]{1,0:T(8,128)}) custom-call(f32[1280,2048]{1,0:T(8,128)} %get-tuple-element.45.refs_0_, f32[1280,384]{1,0:T(8,128)} %get-tuple-element.46.refs_1_, f32[384,65536]{1,0:T(8,128)} %get-tuple-element.38.refs_2_, f32[384,65536]{1,0:T(8,128)} %get-tuple-element.47.refs_3_), custom_call_target="tpu_custom_call", output_to_operand_aliasing={{1}: (3, {})} | custom-call | flops 2013265920 | bytes 25165824 | tf_op jit(solution)/shard_map/wgrad/pallas_call | solution.py:722
  387.8 0.6 slice_reduce_fusion
  (8 shorter events, 0.1 us)
Async XLA Ops:
  3.0 4.7 %copy-start.6 = (bf16[2048]{0:T(1024)(128)(2,1)S(1)}, bf16[2048]{0:T(1024)(128)(2,1)}, u32[]{:S(2)}) copy-start(bf16[2048]{0:T(1024)(128)(2,1)} %param.28) | copy-start | bytes 12292
  3.0 4.7 %copy-start.8 = (bf16[2048,384]{1,0:T(8,128)(2,1)S(1)}, bf16[2048,384]{1,0:T(8,128)(2,1)}, u32[]{:S(2)}) copy-start(bf16[2048,384]{1,0:T(8,128)(2,1)} %param.29) | copy-start | bytes 4718596
  7.6 5.7 %copy-start.7 = (bf16[384]{0:T(512)(128)(2,1)S(1)}, bf16[384]{0:T(512)(128)(2,1)}, u32[]{:S(2)}) copy-start(bf16[384]{0:T(512)(128)(2,1)} %param.23) | copy-start | bytes 2308
  7.7 5.7 %copy-start.2 = (bf16[160,1536]{1,0:T(8,128)(2,1)S(1)}, bf16[160,1536]{1,0:T(8,128)(2,1)}, u32[]{:S(2)}) copy-start(bf16[160,1536]{1,0:T(8,128)(2,1)} %param.16) | copy-start | bytes 1474564
  13.6 1.3 copy-start.5
  13.6 1.3 copy-start.4
  14.8 13.6 %copy-start.1 = (bf16[2048,384]{1,0:T(8,128)(2,1)S(1)}, bf16[2048,384]{1,0:T(8,128)(2,1)}, u32[]{:S(2)}) copy-start(bf16[2048,384]{1,0:T(8,128)(2,1)} %wo_hbm.1) | copy-start | bytes 4718596
  49.1 2.0 copy-start
  334.6 36.3 %copy-start.3 = (f32[1,4480]{1,0:T(1,128)S(1)}, f32[1,4480]{1,0:T(1,128)}, u32[]{:S(2)}) copy-start(f32[1,4480]{1,0:T(1,128)} %get-tuple-element.43) | copy-start | bytes 53764
where the time goes:
time: 389 us; the launch traced here: 388 us
  Pallas kernels  352 us (90%)
  matrix products  24.6 us (6%)
  local copies, waits for them, and re-layouts  6.27 us (2%)
  other arithmetic  4.29 us (1%)
    pallas_call x1, Pallas kernels, proto_grads(): pl.pallas_call(functools.partial(grads_kernel, n_vp, n_dp), out_shape=(ja...  124 us
    pallas_call x3, Pallas kernels, wgrad(): pl.pallas_call(functools.partial(wgrad_kernel, first, n_step, start), gri...  99.2 us
    pallas_call x1, Pallas kernels, sinkhorn_stats(): pl.pallas_call(functools.partial(stats_kernel, n_vp, n_dp), out_shape=(ja...  65.7 us
    pallas_call x1, Pallas kernels, head_pass(): pl.pallas_call(head_kernel, out_shape=(wide, wide, wide, wide, jax.ShapeD...  43.7 us
    pallas_call x1, Pallas kernels, gather_dp(): pl.pallas_call(functools.partial(gather_kernel, n_dp), out_shape=jax.Shap...  19.4 us
    dot_general x1, matrix products, mlp_forward(): jnp.dot(hid_one, w_mid, preferred_element_type=F32) + b_mid.astype(F32)  13.6 us

commit v1 on v0

--- a/solution.py
+++ b/solution.py
@@ -13,7 +13,7 @@
 TEMP_TEACHER = 0.04
 LOG2E = 1.4426950408889634
 LANES = 128
-NB_A = 512
+NB_A = 1024
 NB_B = 1024
 OUT_SLOTS = 3
 HB = 256
@@ -147,85 +147,102 @@
         peer = (me + k) % n_dev
         pl.semaphore_signal(barrier, inc=1, device_id=(peer // n_dp, peer % n_dp), device_id_type=MESH)
 
-    def load(j, slot):
+    def load(which, j):
+        src, buf = ((v_hbm, vbuf), (vt_hbm, tbuf))[which]
         cols = pl.ds(pl.multiple_of(base + j * NB_A, NB_A), NB_A)
-        return (pltpu.make_async_copy(v_hbm.at[:, cols], vbuf.at[slot], in_sem.at[0, slot]),
-                pltpu.make_async_copy(vt_hbm.at[:, cols], tbuf.at[slot], in_sem.at[1, slot]))
-
-    for copy in load(0, 0):
-        copy.start()
+        return pltpu.make_async_copy(src.at[:, cols], buf.at[j % 2], in_sem.at[which, j % 2])
+
+    load(1, 0).start()
+    load(0, 0).start()
     acc_s[...] = jnp.zeros_like(acc_s)
     acc_r[...] = jnp.zeros_like(acc_r)
     ge_ref[...] = jnp.zeros_like(ge_ref)
 
     @pl.loop(0, n_blk)
     def _(j):
-        slot = j % 2
-
         @pl.when(j + 1 < n_blk)
         def _():
-            for copy in load(j + 1, 1 - slot):
-                copy.start()
-
-        for copy in load(j, slot):
-            copy.wait()
-        here = pl.ds(pl.multiple_of(j * NB_A, NB_A), NB_A)
-        unit_t = unit_columns(tbuf[slot])[0].astype(BF16)
+            load(1, j + 1).start()
+
+        load(1, j).wait()
+        unit_t = unit_columns(tbuf[j % 2])[0].astype(BF16)
         kern = jnp.exp2(dot(zt_ref[...], unit_t) * (LOG2E / TEMP_TEACHER))
-        kbuf[:, here] = kern
+        kbuf[:, pl.ds(pl.multiple_of(j * NB_A, NB_A), NB_A)] = kern
         acc_r[...] += fold_lanes(kern * (1.0 / jnp.sum(kern, axis=0, keepdims=True)))
-        unit = unit_columns(vbuf[slot])[0].astype(BF16)
-        ubuf[:, here] = unit
-        exp_s = jnp.exp2(dot(zs_ref[...], unit) * (LOG2E / TEMP_STUDENT))
-        acc_s[...] += fold_lanes(exp_s)
-        ge_ref[...] += dot_t(exp_s.astype(BF16), unit)
 
     pl.semaphore_wait(barrier, n_dev - 1)
 
-    def exchange(step, width):
-        def copy(k, dst, peer):
-            return pltpu.make_async_remote_copy(
-                src_ref=snd.at[step, :, :width], dst_ref=rcv.at[step, dst, :, :width],
-                send_sem=send_sem.at[step, k], recv_sem=recv_sem.at[step, dst],
-                device_id=(peer // n_dp, peer % n_dp), device_id_type=MESH)
+    def message(step, k, dst, peer, width):
+        return pltpu.make_async_remote_copy(
+            src_ref=snd.at[step, :, :width], dst_ref=rcv.at[step, dst, :, :width],
+            send_sem=send_sem.at[step, k], recv_sem=recv_sem.at[step, dst],
+            device_id=(peer // n_dp, peer % n_dp), device_id_type=MESH)
+
+    def publish(step, value):
+        width = value.shape[1]
+        snd[step, :, :width] = value
         for k in range(1, n_dev):
-            copy(k, me, (me + k) % n_dev).start()
-        rcv[step, me, :, :width] = snd[step, :, :width]
+            message(step, k, me, (me + k) % n_dev, width).start()
+        rcv[step, me, :, :width] = value
+
+    def collect(step, width):
         for k in range(1, n_dev):
             src = (me + n_dev - k) % n_dev
-            copy(k, src, src).wait()
+            message(step, k, src, src, width).wait()
         total = rcv[step, 0, :, :width]
         for k in range(1, n_dev):
             total = total + rcv[step, k, :, :width]
         return total
 
-    snd[0, :, :rows_t] = to_row(acc_r[...])
-    snd[0, :, rows_t:rows_t + rows] = to_row(acc_s[...])
-    total = exchange(0, rows_t + rows)
-    row_sum = total[:, rows_t:]
-    rs_ref[...] = row_sum
-    r_row = 1.0 / total[:, :rows_t]
-
-    for step in (1, 2):
+    def rescale(r_row, keep):
         r_col = to_column(r_row)
         acc_r[...] = jnp.zeros_like(acc_r)
-
-        @pl.loop(0, n_col // LANES)
+        span = 4 * LANES
+
+        @pl.loop(0, n_col // span)
         def _(j):
-            here = pl.ds(pl.multiple_of(j * LANES, LANES), LANES)
-            kern = kbuf[:, here]
-            c_row = 1.0 / jnp.sum(kern * r_col, axis=0, keepdims=True)
-            acc_r[...] += kern * c_row
-            if step == 2:
-                c_ref[dp, :, here] = c_row
-
-        if step == 2:
+            total = acc_r[...]
+            for k in range(4):
+                here = pl.ds(pl.multiple_of(j * span + k * LANES, LANES), LANES)
+                kern = kbuf[:, here]
+                c_row = 1.0 / jnp.sum(kern * r_col, axis=0, keepdims=True)
+                total = total + kern * c_row
+                if keep:
+                    c_ref[dp, :, here] = c_row
+            acc_r[...] = total
+
+    third = (n_blk * 3) // 8
+    publish(0, to_row(acc_r[...]))
+
+    @pl.loop(0, n_blk)
+    def _(j):
+        @pl.when(j + 1 < n_blk)
+        def _():
+            load(0, j + 1).start()
+
+        @pl.when(j == third)
+        def _():
+            rescale(1.0 / collect(0, rows_t), False)
+            publish(1, to_row(acc_r[...]))
+
+        @pl.when(j == 2 * third)
+        def _():
+            rescale(1.0 / collect(1, rows_t), True)
+            publish(2, to_row(acc_r[...]))
             for k in range(1, n_dp):
                 pltpu.make_async_remote_copy(
                     src_ref=c_ref.at[dp], dst_ref=c_ref.at[dp], send_sem=c_out.at[k], recv_sem=c_in.at[dp],
                     device_id=(vp, (dp + k) % n_dp), device_id_type=MESH).start()
-        snd[step, :, :rows_t] = to_row(acc_r[...])
-        r_row = 1.0 / exchange(step, rows_t)
+
+        load(0, j).wait()
+        unit = unit_columns(vbuf[j % 2])[0].astype(BF16)
+        ubuf[:, pl.ds(pl.multiple_of(j * NB_A, NB_A), NB_A)] = unit
+        exp_s = jnp.exp2(dot(zs_ref[...], unit) * (LOG2E / TEMP_STUDENT))
+        acc_s[...] += fold_lanes(exp_s)
+        ge_ref[...] += dot_t(exp_s.astype(BF16), unit)
+
+    publish(3, to_row(acc_s[...]))
+    r_row = 1.0 / collect(2, rows_t)
     r_ref[...] = r_row
 
     r_col = to_column(r_row)
@@ -238,9 +255,11 @@
         q_mat = kbuf[:, here] * c_ref[dp, :, here] * r_wide
         q_hi = q_mat.astype(BF16)
         q_lo = (q_mat - q_hi.astype(F32)).astype(BF16)
-        unit = ubuf[:, here]
-        wbuf[...] += dot_t(q_hi, unit) + dot_t(q_lo, unit)
-
+        both = dot_t(jnp.concatenate([q_hi, q_lo], axis=0), ubuf[:, here])
+        wbuf[...] += both[:rows_t] + both[rows_t:]
+
+    row_sum = collect(3, rows)
+    rs_ref[...] = row_sum
     w_zero = wbuf[:n_img]
     w_one = wbuf[n_img:]
     w_both = w_zero + w_one
@@ -291,10 +310,10 @@
             pltpu.VMEM((rows, LANES), F32),
             pltpu.VMEM((rows_t, LANES), F32),
             pltpu.VMEM((rows_t, width), F32),
-            pltpu.VMEM((3, 1, rows + rows_t), F32),
-            pltpu.VMEM((3, n_dev, 1, rows + rows_t), F32),
-            pltpu.SemaphoreType.DMA((3, n_dev)),
-            pltpu.SemaphoreType.DMA((3, n_dev)),
+            pltpu.VMEM((4, 1, rows), F32),
+            pltpu.VMEM((4, n_dev, 1, rows), F32),
+            pltpu.SemaphoreType.DMA((4, n_dev)),
+            pltpu.SemaphoreType.DMA((4, n_dev)),
             pltpu.SemaphoreType.DMA((n_dp,)),
             pltpu.SemaphoreType.DMA((n_dp,)),
         ],

time: 389 us -> 374 us (0.961)
  Pallas kernels: 352 us -> 337 us
    pallas_call x1, Pallas kernels: 65.7 us -> 48.7 us  [sinkhorn_stats(): pl.pallas_call(functools.partial(stats_kernel, n_vp, n_dp), out_shape=(ja...]
where the time goes in v1:
time: 374 us; the launch traced here: 373 us
  Pallas kernels  337 us (90%)
  matrix products  24.6 us (7%)
  local copies, waits for them, and re-layouts  6.27 us (2%)
  other arithmetic  4.29 us (1%)
    pallas_call x1, Pallas kernels, proto_grads(): pl.pallas_call(functools.partial(grads_kernel, n_vp, n_dp), out_shape=(ja...  126 us
    pallas_call x3, Pallas kernels, wgrad(): pl.pallas_call(functools.partial(wgrad_kernel, first, n_step, start), gri...  99.2 us
    pallas_call x1, Pallas kernels, sinkhorn_stats(): pl.pallas_call(functools.partial(stats_kernel, n_vp, n_dp), out_shape=(ja...  48.7 us
    pallas_call x1, Pallas kernels, head_pass(): pl.pallas_call(head_kernel, out_shape=(wide, wide, wide, wide, jax.ShapeD...  43.7 us
    pallas_call x1, Pallas kernels, gather_dp(): pl.pallas_call(functools.partial(gather_kernel, n_dp), out_shape=jax.Shap...  19.4 us
    dot_general x1, matrix products, mlp_forward(): jnp.dot(hid_one, w_mid, preferred_element_type=F32) + b_mid.astype(F32)  13.6 us

profile of v1, /device:TPU:0, one launch (start us, length us, event | category | flops | bytes accessed | tf_op | source)
XLA Modules:
  0.0 373.1 jit_solution(1953181431152005889)
XLA Ops:
  0.6 0.7 convert_element_type.46
  1.3 0.9 reshape.67
  2.3 0.7 convert_element_type.42
  3.0 0.0 copy-start.6
  3.0 0.0 copy-start.8
  3.0 4.6 %fusion.56 = bf16[32,2048]{1,0:T(8,128)(2,1)S(1)} fusion(bf16[32,1536]{1,0:T(8,128)(2,1)S(1)} %bitcast.34, bf16[1536,2048]{1,0:T(8,128)(2,1)} %param.25, f32[2048]{0:T(1024)S(1)} %convert_element_type.42), kind=kOutput, calls=%fused_computation.81 | convolution fusion | flops 205651968 | bytes 6529024 | tf_op jit(solution)/shard_map/dot_general | solution.py:28
  7.6 0.0 copy-done.6
  7.6 0.0 copy-done.8
  7.6 0.0 copy-start.7
  7.7 0.0 copy-start.2
  7.7 5.6 %multiply_reduce_fusion.1 = (f32[32]{0:T(128)S(1)}, f32[32,384]{1,0:T(8,128)S(1)}) fusion(f32[384]{0:T(512)S(1)} %convert_element_type.46, bf16[2048,384]{1,0:T(8,128)(2,1)S(1)} %copy-done.8, bf16[32,2048]{1,0:T(8,128)(2,1)S(1)} %fusion.56, bf16[2048,2048]{1,0:T(8,128)(2,1)} %param.27, f32[2048]{0:T(1024)S(1)} %convert_element_type.44), kind=kOutput, calls=%fused_computation.148 | convolution fusion | flops 323129312 | bytes 10151552 | tf_op jit(solution)/shard_map/dot_general | solution.py:32
  13.3 0.1 broadcast_multiply_fusion.1
  13.4 0.0 copy-done.7
  13.4 0.0 copy-done.2
  13.4 0.2 reshape.65
  13.6 0.0 copy-start.5
  13.6 0.0 copy-start.4
  13.6 1.2 bitcast_convert_fusion
  14.8 0.0 copy-done.5
  14.8 0.0 copy-done.4
  14.8 0.0 copy-start.1
  14.9 13.6 %fusion.5 = bf16[160,2048]{1,0:T(8,128)(2,1)S(1)} fusion(bf16[2048,2048]{1,0:T(8,128)(2,1)} %wm_hbm.1, bf16[160,1536]{1,0:T(8,128)(2,1)S(1)} %bitcast.32, bf16[1536,2048]{1,0:T(8,128)(2,1)} %wi_hbm.1, f32[2048]{0:T(1024)S(1)} %convert_element_type.39, f32[2048]{0:T(1024)S(1)} %convert_element_type.37), kind=kOutput, calls=%fused_computation.11 | convolution fusion | flops 2392064000 | bytes 15843328 | tf_op jit(solution)/shard_map/dot_general | solution.py:30
  28.4 0.0 copy-done.1
  28.4 0.8 multiply_reduce_fusion
  29.3 0.1 broadcast_multiply_fusion
  29.4 19.4 %gather_dp.1 = f32[12,128,384]{2,1,0:T(8,128)S(1)} custom-call(f32[12,16,384]{2,1,0:T(8,128)S(1)} %bitcast.23), custom_call_target="tpu_custom_call" | custom-call | tf_op jit(solution)/shard_map/gather_dp/pallas_call | solution.py:122
  48.8 0.2 convert_element_type.47
  49.0 0.1 slice.40
  49.1 0.0 copy-start
  49.1 1.3 copy.33
  50.4 0.7 slice.41
  51.1 0.0 copy-done
  51.1 48.7 %sinkhorn_stats.1 = (f32[8,1,8192]{2,1,0:T(1,128)}, f32[1,1280]{1,0:T(1,128)}, f32[1,256]{1,0:T(1,128)}, f32[1280,384]{1,0:T(8,128)}, f32[1,128]{1,0:T(1,128)}) custom-call(bf16[1280,384]{1,0:T(8,128)(2,1)} %bitcast.25, bf16[256,384]{1,0:T(8,128)(2,1)} %bitcast.30, bf16[384,65536]{1,0:T(8,128)(2,1)} %v_hbm.3, bf16[384,65536]{1,0:T(8,128)(2,1)} %vt_hbm.3), custom_call_target="tpu_custom_call" | custom-call | flops 16106127360 | bytes 12582912 | tf_op jit(solution)/shard_map/sinkhorn_stats/pallas_call | solution.py:295
  99.8 126.1 %proto_grads.1 = (f32[384,65536]{1,0:T(8,128)}, f32[1280,384]{1,0:T(8,128)}, f32[1,128]{1,0:T(1,128)}, f32[10,128,1536]{2,1,0:T(8,128)}) custom-call(bf16[1280,384]{1,0:T(8,128)(2,1)} %bitcast.26, bf16[384,1280]{1,0:T(8,128)(2,1)} %bitcast.29, bf16[256,384]{1,0:T(8,128)(2,1)} %bitcast.31, f32[1,1280]{1,0:T(1,128)} %get-tuple-element.29.rs_ref, ...), custom_call_target="tpu_custom_call" | custom-call | flops 64424509440 | bytes 100663296 | tf_op jit(solution)/shard_map/proto_grads/pallas_call | solution.py:506
  225.9 1.3 reduce_sum.29
  227.2 0.6 reshape.71.bi_ref
  227.8 0.6 reshape.72.bm_ref
  228.4 0.6 reshape.73.bo_ref
  229.0 43.7 %head_pass.1 = (f32[1280,2048]{1,0:T(8,128)}, f32[1280,2048]{1,0:T(8,128)}, f32[1280,2048]{1,0:T(8,128)}, f32[1280,2048]{1,0:T(8,128)}, f32[1280,384]{1,0:T(8,128)}, /*index=5*/f32[1,4480]{1,0:T(1,128)}) custom-call(f32[1280,1536]{1,0:T(8,128)} %bitcast.27, bf16[1536,2048]{1,0:T(8,128)(2,1)} %wi_hbm.1, bf16[2048,2048]{1,0:T(8,128)(2,1)} %wm_hbm.1, ...), custom_call_target="tpu_custom_call" | custom-call | flops 29527900160 | bytes 41943040 | tf_op jit(solution)/shard_map/head_pass/pallas_call | solution.py:663
  272.7 46.6 %wgrad.3 = (f32[2048,2048]{1,0:T(8,128)}, f32[384,65536]{1,0:T(8,128)}) custom-call(f32[1280,2048]{1,0:T(8,128)} %get-tuple-element.39.refs_0_, f32[1280,2048]{1,0:T(8,128)} %get-tuple-element.40.refs_1_, f32[384,65536]{1,0:T(8,128)} %get-tuple-element.38.refs_2_), custom_call_target="tpu_custom_call" | custom-call | flops 10737418240 | bytes 100663296 | tf_op jit(solution)/shard_map/wgrad/pallas_call | solution.py:741
  319.3 0.0 copy-start.3
  319.3 36.2 %wgrad.4 = (f32[1536,2048]{1,0:T(8,128)}, f32[384,65536]{1,0:T(8,128)}) custom-call(f32[1280,1536]{1,0:T(8,128)} %bitcast.28, f32[1280,2048]{1,0:T(8,128)} %get-tuple-element.37.refs_1_, f32[384,65536]{1,0:T(8,128)} %get-tuple-element.38.refs_2_, f32[384,65536]{1,0:T(8,128)} %get-tuple-element.41.refs_3_), custom_call_target="tpu_custom_call", output_to_operand_aliasing={{1}: (3, {})} | custom-call | flops 8053063680 | bytes 75497472 | tf_op jit(solution)/shard_map/wgrad/pallas_call | solution.py:741
  355.6 0.0 copy-done.3
  355.6 0.6 fusion.165
  356.2 16.3 %wgrad.5 = (f32[2048,384]{1,0:T(8,128)}, f32[384,65536]{1,0:T(8,128)}) custom-call(f32[1280,2048]{1,0:T(8,128)} %get-tuple-element.45.refs_0_, f32[1280,384]{1,0:T(8,128)} %get-tuple-element.46.refs_1_, f32[384,65536]{1,0:T(8,128)} %get-tuple-element.38.refs_2_, f32[384,65536]{1,0:T(8,128)} %get-tuple-element.47.refs_3_), custom_call_target="tpu_custom_call", output_to_operand_aliasing={{1}: (3, {})} | custom-call | flops 2013265920 | bytes 25165824 | tf_op jit(solution)/shard_map/wgrad/pallas_call | solution.py:741
  372.5 0.6 slice_reduce_fusion
  (8 shorter events, 0.1 us)
Async XLA Ops:
  3.0 4.7 %copy-start.6 = (bf16[2048]{0:T(1024)(128)(2,1)S(1)}, bf16[2048]{0:T(1024)(128)(2,1)}, u32[]{:S(2)}) copy-start(bf16[2048]{0:T(1024)(128)(2,1)} %param.28) | copy-start | bytes 12292
  3.0 4.7 %copy-start.8 = (bf16[2048,384]{1,0:T(8,128)(2,1)S(1)}, bf16[2048,384]{1,0:T(8,128)(2,1)}, u32[]{:S(2)}) copy-start(bf16[2048,384]{1,0:T(8,128)(2,1)} %param.29) | copy-start | bytes 4718596
  7.6 5.7 %copy-start.7 = (bf16[384]{0:T(512)(128)(2,1)S(1)}, bf16[384]{0:T(512)(128)(2,1)}, u32[]{:S(2)}) copy-start(bf16[384]{0:T(512)(128)(2,1)} %param.23) | copy-start | bytes 2308
  7.7 5.7 %copy-start.2 = (bf16[160,1536]{1,0:T(8,128)(2,1)S(1)}, bf16[160,1536]{1,0:T(8,128)(2,1)}, u32[]{:S(2)}) copy-start(bf16[160,1536]{1,0:T(8,128)(2,1)} %param.16) | copy-start | bytes 1474564
  13.6 1.3 copy-start.5
  13.6 1.3 copy-start.4
  14.8 13.6 %copy-start.1 = (bf16[2048,384]{1,0:T(8,128)(2,1)S(1)}, bf16[2048,384]{1,0:T(8,128)(2,1)}, u32[]{:S(2)}) copy-start(bf16[2048,384]{1,0:T(8,128)(2,1)} %wo_hbm.1) | copy-start | bytes 4718596
  49.1 2.0 copy-start
  319.3 36.3 %copy-start.3 = (f32[1,4480]{1,0:T(1,128)S(1)}, f32[1,4480]{1,0:T(1,128)}, u32[]{:S(2)}) copy-start(f32[1,4480]{1,0:T(1,128)} %get-tuple-element.43) | copy-start | bytes 53764

commit v2 on v1

--- a/solution.py
+++ b/solution.py
@@ -16,7 +16,8 @@
 NB_A = 1024
 NB_B = 1024
 OUT_SLOTS = 3
-HB = 256
+HB = 512
+RING = 4
 F32 = jnp.float32
 BF16 = jnp.bfloat16
 MESH = pl.DeviceIdType.MESH
@@ -318,7 +319,7 @@
             pltpu.SemaphoreType.DMA((n_dp,)),
         ],
         compiler_params=pltpu.CompilerParams(
-            collective_id=1, has_side_effects=True, vmem_limit_bytes=60 << 20),
+            collective_id=1, has_side_effects=True, vmem_limit_bytes=63 << 20),
         cost_estimate=pl.CostEstimate(flops=flops, bytes_accessed=4 * width * n_col, transcendentals=rows * n_col),
         name="sinkhorn_stats",
     )(z_s, z_t, protos, ema_protos)
@@ -446,7 +447,7 @@
             for k in range(1, n_dev):
                 total = total + part_ge[k]
                 loss = loss + part_loss[k]
-            loss_all[...] = loss
+            loss_all[...] = jnp.sum(loss, axis=1, keepdims=True)
             sum_ge[...] = total
             ge_all[pl.ds(pl.multiple_of(me * n_own, n_own), n_own)] = total
 
@@ -507,7 +508,7 @@
         functools.partial(grads_kernel, n_vp, n_dp),
         out_shape=(jax.ShapeDtypeStruct((width, n_col), F32),
                    jax.ShapeDtypeStruct((rows, width), F32),
-                   jax.ShapeDtypeStruct((1, LANES), F32),
+                   jax.ShapeDtypeStruct((1, 1), F32),
                    jax.ShapeDtypeStruct((x_loc.shape[0], x_loc.shape[1] * n_dp, x_loc.shape[2]), F32)),
         in_specs=[VMEM] * 9 + [HBM] * 2,
         out_specs=(HBM, VMEM, VMEM, HBM),
@@ -524,7 +525,7 @@
             dma((n_blk,)),
         ] + [dma((n_dev,))] * 6 + [dma((n_dp // 2,))] * 4 + [dma((1,))],
         compiler_params=pltpu.CompilerParams(
-            collective_id=2, has_side_effects=True, vmem_limit_bytes=60 << 20),
+            collective_id=2, has_side_effects=True, vmem_limit_bytes=63 << 20),
         cost_estimate=pl.CostEstimate(
             flops=2 * rows * n_col * width, bytes_accessed=4 * width * n_col, transcendentals=rows * n_col // 2),
         name="proto_grads",
@@ -702,23 +703,24 @@
         return pl.ds(pl.multiple_of(base + step * chunk, chunk), chunk)
 
     def read(step):
-        return pltpu.make_async_copy(src.at[:, cols(step)], cbuf.at[step % 3], rd_sem.at[step % 3])
+        return pltpu.make_async_copy(src.at[:, cols(step)], cbuf.at[step % RING], rd_sem.at[step % RING])
 
     def write(step):
-        return pltpu.make_async_copy(cbuf.at[step % 3], dst.at[:, cols(step)], wr_sem.at[step % 3])
+        return pltpu.make_async_copy(cbuf.at[step % RING], dst.at[:, cols(step)], wr_sem.at[step % RING])
 
     @pl.when(i == 0)
     def _():
         read(0).start()
+        read(1).start()
         low[...] = b_ref[...].astype(BF16)
 
     @pl.when(i >= 2)
     def _():
         write(i - 2).wait()
 
-    @pl.when(i + 1 < n_step)
+    @pl.when(i + 2 < n_step)
     def _():
-        read(i + 1).start()
+        read(i + 2).start()
 
     read(i).wait()
     write(i).start()
@@ -747,11 +749,11 @@
                   HBM] + ([] if first else [HBM]),
         out_specs=(pl.BlockSpec((block, n_right), lambda i: (i, 0)), HBM),
         scratch_shapes=[pltpu.VMEM((rows, n_right), BF16),
-                        pltpu.VMEM((3, src.shape[0], chunk), F32),
-                        pltpu.SemaphoreType.DMA((3,)), pltpu.SemaphoreType.DMA((3,))],
+                        pltpu.VMEM((RING, src.shape[0], chunk), F32),
+                        pltpu.SemaphoreType.DMA((RING,)), pltpu.SemaphoreType.DMA((RING,))],
         input_output_aliases={} if first else {3: 1},
         compiler_params=pltpu.CompilerParams(
-            dimension_semantics=("arbitrary",), vmem_limit_bytes=60 << 20),
+            dimension_semantics=("arbitrary",), vmem_limit_bytes=63 << 20),
         cost_estimate=pl.CostEstimate(
             flops=2 * rows * n_left * n_right, bytes_accessed=8 * src.shape[0] * width, transcendentals=0),
         name="wgrad",
@@ -787,7 +789,7 @@
         g_w_out, g_protos = wgrad(hid_two, g_proj, g_temp, g_protos, 7 * part, part)
         biases = biases.reshape(-1)
         g_b_mid, g_b_in, g_b_out = biases[:n_hid], biases[n_hid:2 * n_hid], biases[2 * n_hid:]
-        return (jnp.sum(loss), g_w_in, g_b_in, g_w_mid, g_b_mid, g_w_out, g_b_out, g_protos)
+        return (loss.reshape(()), g_w_in, g_b_in, g_w_mid, g_b_mid, g_w_out, g_b_out, g_protos)
 
     by_rows = P('dp', None)
     by_cols = P(None, 'vp')

time: 374 us -> 372 us (level)
  no operation moved by 1% of the time
where the time goes in v2:
time: 372 us; the launch traced here: 371 us
  Pallas kernels  334 us (90%)
  matrix products  24.7 us (7%)
  local copies, waits for them, and re-layouts  6.3 us (2%)
    pallas_call x1, Pallas kernels, proto_grads(): pl.pallas_call(functools.partial(grads_kernel, n_vp, n_dp), out_shape=(ja...  126 us
    pallas_call x3, Pallas kernels, wgrad(): pl.pallas_call(functools.partial(wgrad_kernel, first, n_step, start), gri...  97.7 us
    pallas_call x1, Pallas kernels, sinkhorn_stats(): pl.pallas_call(functools.partial(stats_kernel, n_vp, n_dp), out_shape=(ja...  48.6 us
    pallas_call x1, Pallas kernels, head_pass(): pl.pallas_call(head_kernel, out_shape=(wide, wide, wide, wide, jax.ShapeD...  42.6 us
    pallas_call x1, Pallas kernels, gather_dp(): pl.pallas_call(functools.partial(gather_kernel, n_dp), out_shape=jax.Shap...  19.4 us
    dot_general x1, matrix products, mlp_forward(): jnp.dot(hid_one, w_mid, preferred_element_type=F32) + b_mid.astype(F32)  13.6 us

profile of v2, /device:TPU:0, one launch (start us, length us, event | category | flops | bytes accessed | tf_op | source)
XLA Modules:
  0.0 371.1 jit_solution(9797879900171262524)
XLA Ops:
  0.6 0.7 convert_element_type.46
  1.3 0.9 reshape.70
  2.3 0.7 convert_element_type.42
  3.0 0.0 copy-start.8
  3.0 0.0 copy-start.11
  3.0 4.6 %fusion.56 = bf16[32,2048]{1,0:T(8,128)(2,1)S(1)} fusion(bf16[32,1536]{1,0:T(8,128)(2,1)S(1)} %bitcast.35, bf16[1536,2048]{1,0:T(8,128)(2,1)} %param.25, f32[2048]{0:T(1024)S(1)} %convert_element_type.42), kind=kOutput, calls=%fused_computation.81 | convolution fusion | flops 205651968 | bytes 6529024 | tf_op jit(solution)/shard_map/dot_general | solution.py:29
  7.6 0.0 copy-done.8
  7.6 0.0 copy-done.11
  7.6 0.0 copy-start.9
  7.7 0.0 copy-start.2
  7.7 5.6 %multiply_reduce_fusion.1 = (f32[32]{0:T(128)S(1)}, f32[32,384]{1,0:T(8,128)S(1)}) fusion(f32[384]{0:T(512)S(1)} %convert_element_type.46, bf16[2048,384]{1,0:T(8,128)(2,1)S(1)} %copy-done.11, bf16[32,2048]{1,0:T(8,128)(2,1)S(1)} %fusion.56, bf16[2048,2048]{1,0:T(8,128)(2,1)} %param.27, f32[2048]{0:T(1024)S(1)} %convert_element_type.44), kind=kOutput, calls=%fused_computation.148 | convolution fusion | flops 323129312 | bytes 10151552 | tf_op jit(solution)/shard_map/dot_general | solution.py:33
  13.3 0.1 broadcast_multiply_fusion.1
  13.4 0.0 copy-done.9
  13.4 0.0 copy-done.2
  13.4 0.2 reshape.68
  13.6 0.0 copy-start.6
  13.6 0.0 copy-start.4
  13.6 1.2 bitcast_convert_fusion
  14.8 0.0 copy-done.6
  14.9 0.0 copy-done.4
  14.9 0.0 copy-start.1
  14.9 13.6 %fusion.5 = bf16[160,2048]{1,0:T(8,128)(2,1)S(1)} fusion(bf16[2048,2048]{1,0:T(8,128)(2,1)} %wm_hbm.1, bf16[160,1536]{1,0:T(8,128)(2,1)S(1)} %bitcast.33, bf16[1536,2048]{1,0:T(8,128)(2,1)} %wi_hbm.1, f32[2048]{0:T(1024)S(1)} %convert_element_type.39, f32[2048]{0:T(1024)S(1)} %convert_element_type.37), kind=kOutput, calls=%fused_computation.11 | convolution fusion | flops 2392064000 | bytes 15843328 | tf_op jit(solution)/shard_map/dot_general | solution.py:31
  28.5 0.0 copy-done.1
  28.5 0.8 multiply_reduce_fusion
  29.4 0.1 broadcast_multiply_fusion
  29.5 19.4 %gather_dp.1 = f32[12,128,384]{2,1,0:T(8,128)S(1)} custom-call(f32[12,16,384]{2,1,0:T(8,128)S(1)} %bitcast.24), custom_call_target="tpu_custom_call" | custom-call | tf_op jit(solution)/shard_map/gather_dp/pallas_call | solution.py:123
  48.9 0.2 convert_element_type.47
  49.1 0.1 slice.40
  49.2 0.0 copy-start
  49.2 1.3 copy.33
  50.6 0.7 slice.41
  51.3 0.0 copy-done
  51.3 48.6 %sinkhorn_stats.1 = (f32[8,1,8192]{2,1,0:T(1,128)}, f32[1,1280]{1,0:T(1,128)}, f32[1,256]{1,0:T(1,128)}, f32[1280,384]{1,0:T(8,128)}, f32[1,128]{1,0:T(1,128)}) custom-call(bf16[1280,384]{1,0:T(8,128)(2,1)} %bitcast.26, bf16[256,384]{1,0:T(8,128)(2,1)} %bitcast.31, bf16[384,65536]{1,0:T(8,128)(2,1)} %v_hbm.3, bf16[384,65536]{1,0:T(8,128)(2,1)} %vt_hbm.3), custom_call_target="tpu_custom_call" | custom-call | flops 16106127360 | bytes 12582912 | tf_op jit(solution)/shard_map/sinkhorn_stats/pallas_call | solution.py:296
  99.9 0.0 copy-start.5
  99.9 0.0 copy-start.7
  99.9 0.0 copy-start.10
  99.9 126.2 %proto_grads.1 = (f32[384,65536]{1,0:T(8,128)}, f32[1280,384]{1,0:T(8,128)}, f32[1,1]{1,0:T(1,128)}, f32[10,128,1536]{2,1,0:T(8,128)}) custom-call(bf16[1280,384]{1,0:T(8,128)(2,1)} %bitcast.27, bf16[384,1280]{1,0:T(8,128)(2,1)} %bitcast.30, bf16[256,384]{1,0:T(8,128)(2,1)} %bitcast.32, f32[1,1280]{1,0:T(1,128)} %get-tuple-element.29.rs_ref, ...), custom_call_target="tpu_custom_call" | custom-call | flops 64424509440 | bytes 100663296 | tf_op jit(solution)/shard_map/proto_grads/pallas_call | solution.py:507
  226.1 0.0 copy-done.5
  226.1 0.6 reshape.75.bi_ref
  226.7 0.0 copy-done.7
  226.7 0.6 reshape.76.bm_ref
  227.3 0.0 copy-done.10
  227.3 0.6 reshape.77.bo_ref
  227.9 42.6 %head_pass.1 = (f32[1280,2048]{1,0:T(8,128)}, f32[1280,2048]{1,0:T(8,128)}, f32[1280,2048]{1,0:T(8,128)}, f32[1280,2048]{1,0:T(8,128)}, f32[1280,384]{1,0:T(8,128)}, /*index=5*/f32[1,4480]{1,0:T(1,128)}) custom-call(f32[1280,1536]{1,0:T(8,128)} %bitcast.28, bf16[1536,2048]{1,0:T(8,128)(2,1)} %wi_hbm.1, bf16[2048,2048]{1,0:T(8,128)(2,1)} %wm_hbm.1, ...), custom_call_target="tpu_custom_call" | custom-call | flops 29527900160 | bytes 41943040 | tf_op jit(solution)/shard_map/head_pass/pallas_call | solution.py:664
  270.5 46.1 %wgrad.3 = (f32[2048,2048]{1,0:T(8,128)}, f32[384,65536]{1,0:T(8,128)}) custom-call(f32[1280,2048]{1,0:T(8,128)} %get-tuple-element.39.refs_0_, f32[1280,2048]{1,0:T(8,128)} %get-tuple-element.40.refs_1_, f32[384,65536]{1,0:T(8,128)} %get-tuple-element.38.refs_2_), custom_call_target="tpu_custom_call" | custom-call | flops 10737418240 | bytes 100663296 | tf_op jit(solution)/shard_map/wgrad/pallas_call | solution.py:743
  316.6 0.0 copy-start.3
  316.7 35.9 %wgrad.4 = (f32[1536,2048]{1,0:T(8,128)}, f32[384,65536]{1,0:T(8,128)}) custom-call(f32[1280,1536]{1,0:T(8,128)} %bitcast.29, f32[1280,2048]{1,0:T(8,128)} %get-tuple-element.37.refs_1_, f32[384,65536]{1,0:T(8,128)} %get-tuple-element.38.refs_2_, f32[384,65536]{1,0:T(8,128)} %get-tuple-element.41.refs_3_), custom_call_target="tpu_custom_call", output_to_operand_aliasing={{1}: (3, {})} | custom-call | flops 8053063680 | bytes 75497472 | tf_op jit(solution)/shard_map/wgrad/pallas_call | solution.py:743
  352.6 0.0 copy-done.3
  352.6 0.6 fusion.165
  353.2 15.7 %wgrad.5 = (f32[2048,384]{1,0:T(8,128)}, f32[384,65536]{1,0:T(8,128)}) custom-call(f32[1280,2048]{1,0:T(8,128)} %get-tuple-element.45.refs_0_, f32[1280,384]{1,0:T(8,128)} %get-tuple-element.46.refs_1_, f32[384,65536]{1,0:T(8,128)} %get-tuple-element.38.refs_2_, f32[384,65536]{1,0:T(8,128)} %get-tuple-element.47.refs_3_), custom_call_target="tpu_custom_call", output_to_operand_aliasing={{1}: (3, {})} | custom-call | flops 2013265920 | bytes 25165824 | tf_op jit(solution)/shard_map/wgrad/pallas_call | solution.py:743
  368.8 0.6 slice_reduce_fusion
  (8 shorter events, 0.1 us)
Async XLA Ops:
  3.0 4.7 %copy-start.8 = (bf16[2048]{0:T(1024)(128)(2,1)S(1)}, bf16[2048]{0:T(1024)(128)(2,1)}, u32[]{:S(2)}) copy-start(bf16[2048]{0:T(1024)(128)(2,1)} %param.28) | copy-start | bytes 12292
  3.0 4.7 %copy-start.11 = (bf16[2048,384]{1,0:T(8,128)(2,1)S(1)}, bf16[2048,384]{1,0:T(8,128)(2,1)}, u32[]{:S(2)}) copy-start(bf16[2048,384]{1,0:T(8,128)(2,1)} %param.29) | copy-start | bytes 4718596
  7.6 5.7 %copy-start.9 = (bf16[384]{0:T(512)(128)(2,1)S(1)}, bf16[384]{0:T(512)(128)(2,1)}, u32[]{:S(2)}) copy-start(bf16[384]{0:T(512)(128)(2,1)} %param.23) | copy-start | bytes 2308
  7.7 5.7 %copy-start.2 = (bf16[160,1536]{1,0:T(8,128)(2,1)S(1)}, bf16[160,1536]{1,0:T(8,128)(2,1)}, u32[]{:S(2)}) copy-start(bf16[160,1536]{1,0:T(8,128)(2,1)} %param.16) | copy-start | bytes 1474564
  13.6 1.3 copy-start.6
  13.6 1.3 copy-start.4
  14.9 13.7 %copy-start.1 = (bf16[2048,384]{1,0:T(8,128)(2,1)S(1)}, bf16[2048,384]{1,0:T(8,128)(2,1)}, u32[]{:S(2)}) copy-start(bf16[2048,384]{1,0:T(8,128)(2,1)} %wo_hbm.1) | copy-start | bytes 4718596
  49.2 2.0 copy-start
  99.9 126.2 %copy-start.5 = (bf16[2048]{0:T(1024)(128)(2,1)S(1)}, bf16[2048]{0:T(1024)(128)(2,1)}, u32[]{:S(2)}) copy-start(bf16[2048]{0:T(1024)(128)(2,1)} %param.19) | copy-start | bytes 12292
  99.9 126.8 %copy-start.7 = (bf16[2048]{0:T(1024)(128)(2,1)S(1)}, bf16[2048]{0:T(1024)(128)(2,1)}, u32[]{:S(2)}) copy-start(bf16[2048]{0:T(1024)(128)(2,1)} %param.21) | copy-start | bytes 12292
  99.9 127.4 %copy-start.10 = (bf16[384]{0:T(512)(128)(2,1)S(1)}, bf16[384]{0:T(512)(128)(2,1)}, u32[]{:S(2)}) copy-start(bf16[384]{0:T(512)(128)(2,1)} %param.23) | copy-start | bytes 2308
  316.6 35.9 %copy-start.3 = (f32[1,4480]{1,0:T(1,128)S(1)}, f32[1,4480]{1,0:T(1,128)}, u32[]{:S(2)}) copy-start(f32[1,4480]{1,0:T(1,128)} %get-tuple-element.43) | copy-start | bytes 53764

commit v3 on v2

--- a/solution.py
+++ b/solution.py
@@ -15,7 +15,7 @@
 LANES = 128
 NB_A = 1024
 NB_B = 1024
-OUT_SLOTS = 3
+OUT_SLOTS = 5
 HB = 512
 RING = 4
 F32 = jnp.float32

time: 372 us -> 372 us (level)
  no operation moved by 1% of the time
where the time goes in v3:
time: 372 us; the launch traced here: 371 us
  Pallas kernels  335 us (90%)
  matrix products  24.7 us (7%)
  local copies, waits for them, and re-layouts  6.3 us (2%)
    pallas_call x1, Pallas kernels, proto_grads(): pl.pallas_call(functools.partial(grads_kernel, n_vp, n_dp), out_shape=(ja...  126 us
    pallas_call x3, Pallas kernels, wgrad(): pl.pallas_call(functools.partial(wgrad_kernel, first, n_step, start), gri...  97.7 us
    pallas_call x1, Pallas kernels, sinkhorn_stats(): pl.pallas_call(functools.partial(stats_kernel, n_vp, n_dp), out_shape=(ja...  48.6 us
    pallas_call x1, Pallas kernels, head_pass(): pl.pallas_call(head_kernel, out_shape=(wide, wide, wide, wide, jax.ShapeD...  42.6 us
    pallas_call x1, Pallas kernels, gather_dp(): pl.pallas_call(functools.partial(gather_kernel, n_dp), out_shape=jax.Shap...  19.4 us
    dot_general x1, matrix products, mlp_forward(): jnp.dot(hid_one, w_mid, preferred_element_type=F32) + b_mid.astype(F32)  13.6 us

profile of v3, /device:TPU:0, one launch (start us, length us, event | category | flops | bytes accessed | tf_op | source)
XLA Modules:
  0.0 371.1 jit_solution(14485715367476366307)
XLA Ops:
  0.6 0.7 convert_element_type.46
  1.3 0.9 reshape.70
  2.3 0.7 convert_element_type.42
  3.0 0.0 copy-start.8
  3.0 0.0 copy-start.11
  3.0 4.6 %fusion.56 = bf16[32,2048]{1,0:T(8,128)(2,1)S(1)} fusion(bf16[32,1536]{1,0:T(8,128)(2,1)S(1)} %bitcast.35, bf16[1536,2048]{1,0:T(8,128)(2,1)} %param.25, f32[2048]{0:T(1024)S(1)} %convert_element_type.42), kind=kOutput, calls=%fused_computation.81 | convolution fusion | flops 205651968 | bytes 6529024 | tf_op jit(solution)/shard_map/dot_general | solution.py:29
  7.6 0.0 copy-done.8
  7.6 0.0 copy-done.11
  7.6 0.0 copy-start.9
  7.7 0.0 copy-start.2
  7.7 5.6 %multiply_reduce_fusion.1 = (f32[32]{0:T(128)S(1)}, f32[32,384]{1,0:T(8,128)S(1)}) fusion(f32[384]{0:T(512)S(1)} %convert_element_type.46, bf16[2048,384]{1,0:T(8,128)(2,1)S(1)} %copy-done.11, bf16[32,2048]{1,0:T(8,128)(2,1)S(1)} %fusion.56, bf16[2048,2048]{1,0:T(8,128)(2,1)} %param.27, f32[2048]{0:T(1024)S(1)} %convert_element_type.44), kind=kOutput, calls=%fused_computation.148 | convolution fusion | flops 323129312 | bytes 10151552 | tf_op jit(solution)/shard_map/dot_general | solution.py:33
  13.3 0.1 broadcast_multiply_fusion.1
  13.4 0.0 copy-done.9
  13.4 0.0 copy-done.2
  13.4 0.2 reshape.68
  13.6 0.0 copy-start.6
  13.6 0.0 copy-start.4
  13.6 1.2 bitcast_convert_fusion
  14.8 0.0 copy-done.6
  14.9 0.0 copy-done.4
  14.9 0.0 copy-start.1
  14.9 13.6 %fusion.5 = bf16[160,2048]{1,0:T(8,128)(2,1)S(1)} fusion(bf16[2048,2048]{1,0:T(8,128)(2,1)} %wm_hbm.1, bf16[160,1536]{1,0:T(8,128)(2,1)S(1)} %bitcast.33, bf16[1536,2048]{1,0:T(8,128)(2,1)} %wi_hbm.1, f32[2048]{0:T(1024)S(1)} %convert_element_type.39, f32[2048]{0:T(1024)S(1)} %convert_element_type.37), kind=kOutput, calls=%fused_computation.11 | convolution fusion | flops 2392064000 | bytes 15843328 | tf_op jit(solution)/shard_map/dot_general | solution.py:31
  28.5 0.0 copy-done.1
  28.5 0.8 multiply_reduce_fusion
  29.4 0.1 broadcast_multiply_fusion
  29.5 19.4 %gather_dp.1 = f32[12,128,384]{2,1,0:T(8,128)S(1)} custom-call(f32[12,16,384]{2,1,0:T(8,128)S(1)} %bitcast.24), custom_call_target="tpu_custom_call" | custom-call | tf_op jit(solution)/shard_map/gather_dp/pallas_call | solution.py:123
  48.9 0.2 convert_element_type.47
  49.1 0.1 slice.40
  49.2 0.0 copy-start
  49.2 1.3 copy.33
  50.6 0.7 slice.41
  51.3 0.0 copy-done
  51.3 48.6 %sinkhorn_stats.1 = (f32[8,1,8192]{2,1,0:T(1,128)}, f32[1,1280]{1,0:T(1,128)}, f32[1,256]{1,0:T(1,128)}, f32[1280,384]{1,0:T(8,128)}, f32[1,128]{1,0:T(1,128)}) custom-call(bf16[1280,384]{1,0:T(8,128)(2,1)} %bitcast.26, bf16[256,384]{1,0:T(8,128)(2,1)} %bitcast.31, bf16[384,65536]{1,0:T(8,128)(2,1)} %v_hbm.3, bf16[384,65536]{1,0:T(8,128)(2,1)} %vt_hbm.3), custom_call_target="tpu_custom_call" | custom-call | flops 16106127360 | bytes 12582912 | tf_op jit(solution)/shard_map/sinkhorn_stats/pallas_call | solution.py:296
  99.9 0.0 copy-start.5
  99.9 0.0 copy-start.7
  99.9 0.0 copy-start.10
  99.9 126.2 %proto_grads.1 = (f32[384,65536]{1,0:T(8,128)}, f32[1280,384]{1,0:T(8,128)}, f32[1,1]{1,0:T(1,128)}, f32[10,128,1536]{2,1,0:T(8,128)}) custom-call(bf16[1280,384]{1,0:T(8,128)(2,1)} %bitcast.27, bf16[384,1280]{1,0:T(8,128)(2,1)} %bitcast.30, bf16[256,384]{1,0:T(8,128)(2,1)} %bitcast.32, f32[1,1280]{1,0:T(1,128)} %get-tuple-element.29.rs_ref, ...), custom_call_target="tpu_custom_call" | custom-call | flops 64424509440 | bytes 100663296 | tf_op jit(solution)/shard_map/proto_grads/pallas_call | solution.py:507
  226.2 0.0 copy-done.5
  226.2 0.6 reshape.75.bi_ref
  226.8 0.0 copy-done.7
  226.8 0.6 reshape.76.bm_ref
  227.4 0.0 copy-done.10
  227.4 0.6 reshape.77.bo_ref
  227.9 42.6 %head_pass.1 = (f32[1280,2048]{1,0:T(8,128)}, f32[1280,2048]{1,0:T(8,128)}, f32[1280,2048]{1,0:T(8,128)}, f32[1280,2048]{1,0:T(8,128)}, f32[1280,384]{1,0:T(8,128)}, /*index=5*/f32[1,4480]{1,0:T(1,128)}) custom-call(f32[1280,1536]{1,0:T(8,128)} %bitcast.28, bf16[1536,2048]{1,0:T(8,128)(2,1)} %wi_hbm.1, bf16[2048,2048]{1,0:T(8,128)(2,1)} %wm_hbm.1, ...), custom_call_target="tpu_custom_call" | custom-call | flops 29527900160 | bytes 41943040 | tf_op jit(solution)/shard_map/head_pass/pallas_call | solution.py:664
  270.5 46.1 %wgrad.3 = (f32[2048,2048]{1,0:T(8,128)}, f32[384,65536]{1,0:T(8,128)}) custom-call(f32[1280,2048]{1,0:T(8,128)} %get-tuple-element.39.refs_0_, f32[1280,2048]{1,0:T(8,128)} %get-tuple-element.40.refs_1_, f32[384,65536]{1,0:T(8,128)} %get-tuple-element.38.refs_2_), custom_call_target="tpu_custom_call" | custom-call | flops 10737418240 | bytes 100663296 | tf_op jit(solution)/shard_map/wgrad/pallas_call | solution.py:743
  316.7 0.0 copy-start.3
  316.7 35.9 %wgrad.4 = (f32[1536,2048]{1,0:T(8,128)}, f32[384,65536]{1,0:T(8,128)}) custom-call(f32[1280,1536]{1,0:T(8,128)} %bitcast.29, f32[1280,2048]{1,0:T(8,128)} %get-tuple-element.37.refs_1_, f32[384,65536]{1,0:T(8,128)} %get-tuple-element.38.refs_2_, f32[384,65536]{1,0:T(8,128)} %get-tuple-element.41.refs_3_), custom_call_target="tpu_custom_call", output_to_operand_aliasing={{1}: (3, {})} | custom-call | flops 8053063680 | bytes 75497472 | tf_op jit(solution)/shard_map/wgrad/pallas_call | solution.py:743
  352.6 0.0 copy-done.3
  352.6 0.6 fusion.165
  353.2 15.7 %wgrad.5 = (f32[2048,384]{1,0:T(8,128)}, f32[384,65536]{1,0:T(8,128)}) custom-call(f32[1280,2048]{1,0:T(8,128)} %get-tuple-element.45.refs_0_, f32[1280,384]{1,0:T(8,128)} %get-tuple-element.46.refs_1_, f32[384,65536]{1,0:T(8,128)} %get-tuple-element.38.refs_2_, f32[384,65536]{1,0:T(8,128)} %get-tuple-element.47.refs_3_), custom_call_target="tpu_custom_call", output_to_operand_aliasing={{1}: (3, {})} | custom-call | flops 2013265920 | bytes 25165824 | tf_op jit(solution)/shard_map/wgrad/pallas_call | solution.py:743
  368.9 0.6 slice_reduce_fusion
  (8 shorter events, 0.1 us)
Async XLA Ops:
  3.0 4.7 %copy-start.8 = (bf16[2048]{0:T(1024)(128)(2,1)S(1)}, bf16[2048]{0:T(1024)(128)(2,1)}, u32[]{:S(2)}) copy-start(bf16[2048]{0:T(1024)(128)(2,1)} %param.28) | copy-start | bytes 12292
  3.0 4.7 %copy-start.11 = (bf16[2048,384]{1,0:T(8,128)(2,1)S(1)}, bf16[2048,384]{1,0:T(8,128)(2,1)}, u32[]{:S(2)}) copy-start(bf16[2048,384]{1,0:T(8,128)(2,1)} %param.29) | copy-start | bytes 4718596
  7.6 5.7 %copy-start.9 = (bf16[384]{0:T(512)(128)(2,1)S(1)}, bf16[384]{0:T(512)(128)(2,1)}, u32[]{:S(2)}) copy-start(bf16[384]{0:T(512)(128)(2,1)} %param.23) | copy-start | bytes 2308
  7.7 5.7 %copy-start.2 = (bf16[160,1536]{1,0:T(8,128)(2,1)S(1)}, bf16[160,1536]{1,0:T(8,128)(2,1)}, u32[]{:S(2)}) copy-start(bf16[160,1536]{1,0:T(8,128)(2,1)} %param.16) | copy-start | bytes 1474564
  13.6 1.3 copy-start.6
  13.6 1.3 copy-start.4
  14.9 13.7 %copy-start.1 = (bf16[2048,384]{1,0:T(8,128)(2,1)S(1)}, bf16[2048,384]{1,0:T(8,128)(2,1)}, u32[]{:S(2)}) copy-start(bf16[2048,384]{1,0:T(8,128)(2,1)} %wo_hbm.1) | copy-start | bytes 4718596
  49.2 2.0 copy-start
  99.9 126.2 %copy-start.5 = (bf16[2048]{0:T(1024)(128)(2,1)S(1)}, bf16[2048]{0:T(1024)(128)(2,1)}, u32[]{:S(2)}) copy-start(bf16[2048]{0:T(1024)(128)(2,1)} %param.19) | copy-start | bytes 12292
  99.9 126.9 %copy-start.7 = (bf16[2048]{0:T(1024)(128)(2,1)S(1)}, bf16[2048]{0:T(1024)(128)(2,1)}, u32[]{:S(2)}) copy-start(bf16[2048]{0:T(1024)(128)(2,1)} %param.21) | copy-start | bytes 12292
  99.9 127.4 %copy-start.10 = (bf16[384]{0:T(512)(128)(2,1)S(1)}, bf16[384]{0:T(512)(128)(2,1)}, u32[]{:S(2)}) copy-start(bf16[384]{0:T(512)(128)(2,1)} %param.23) | copy-start | bytes 2308
  316.7 35.9 %copy-start.3 = (f32[1,4480]{1,0:T(1,128)S(1)}, f32[1,4480]{1,0:T(1,128)}, u32[]{:S(2)}) copy-start(f32[1,4480]{1,0:T(1,128)} %get-tuple-element.43) | copy-start | bytes 53764
